TPU v7x, 32 devices: a whole 2x2x4 slice. The times are simulated.
32 devices in a mesh: frame: 16 (over z, y, x), row: 2 (over core).
Axes of the slice: x: 2, y: 2, z: 4, core: 2. Of those that a mesh axis runs over, the one named last changes fastest.
Arguments:
- footage: float32 [64, 1024, 1024], P('frame', 'row'), may hold values from -30 to 30
Outputs:
- coefficients: float32 [64, 1024, 1024], P('frame', 'row')
- energies: float32 [4, 10], replicated
All inputs are finite; a program needn't handle non-finite values.
Results may differ from a plain program's by a relative error of at most 0.00007.
Values sent between devices are 32-bit elements; how exact they have to be, the bound alone decides.
No kernel may reach another device: no remote copies, remote signals or barrier semaphores. Data moves between devices by JAX's collectives and lax.ppermute only.
A program may use at most 128 MiB of HBM per device.

v0:
```python
import jax
import jax.numpy as jnp
import numpy as np
from jax import lax
from jax.sharding import PartitionSpec as P

SLEVELS = 3
TLEVELS = 3


LIFT_ALPHA = -1.586134342
LIFT_BETA = -0.05298011854
LIFT_GAMMA = 0.8829110762
LIFT_DELTA = 0.4435068522
LIFT_ZETA = 1.149604398


def shifted(block, axis, distance):
    devices = range(lax.axis_size(axis))
    route = [(i - distance, i) for i in devices if i - distance in devices]
    return lax.ppermute(block, axis, route)


def mirror_after(values, along):
    length = values.shape[along]
    return jnp.concatenate(
        [
            lax.slice_in_dim(values, 1, length, axis=along),
            lax.slice_in_dim(values, length - 1, length, axis=along),
        ],
        axis=along,
    )


def mirror_before(values, along):
    length = values.shape[along]
    return jnp.concatenate(
        [
            lax.slice_in_dim(values, 0, 1, axis=along),
            lax.slice_in_dim(values, 0, length - 1, axis=along),
        ],
        axis=along,
    )


def weave_axis(even_part, odd_part, along):
    stacked = jnp.stack([even_part, odd_part], axis=along + 1)
    new_shape = list(even_part.shape)
    new_shape[along] = new_shape[along] * 2
    return stacked.reshape(tuple(new_shape))


def lift_pair(even_part, odd_part, take_next, take_prev):
    odd_part = odd_part + LIFT_ALPHA * (even_part + take_next(even_part))
    even_part = even_part + LIFT_BETA * (take_prev(odd_part) + odd_part)
    odd_part = odd_part + LIFT_GAMMA * (even_part + take_next(even_part))
    even_part = even_part + LIFT_DELTA * (take_prev(odd_part) + odd_part)
    return (even_part * LIFT_ZETA, odd_part * (1.0 / LIFT_ZETA))


def table_next(values):
    return np.concatenate([values[:, 1:], values[:, -1:]], axis=1)


def table_prev(values):
    return np.concatenate([values[:, :1], values[:, :-1]], axis=1)


def column_matrix(width):
    identity = np.eye(width)
    even_part = identity[:, 0::2]
    odd_part = identity[:, 1::2]
    odd_part = odd_part + LIFT_ALPHA * (even_part + table_next(even_part))
    even_part = even_part + LIFT_BETA * (table_prev(odd_part) + odd_part)
    odd_part = odd_part + LIFT_GAMMA * (even_part + table_next(even_part))
    even_part = even_part + LIFT_DELTA * (table_prev(odd_part) + odd_part)
    lifted = np.concatenate([even_part * LIFT_ZETA, odd_part * (1.0 / LIFT_ZETA)], axis=1)
    return jnp.asarray(lifted.astype(np.float32))


def spatial_inplace(block, levels):
    frame_count, row_count, width = block.shape
    mixed = jnp.dot(block, column_matrix(width), precision=lax.Precision.HIGHEST)
    paired = mixed.reshape(frame_count, row_count // 2, 2, width)
    low_rows, high_rows = lift_pair(paired[:, :, 0, :], paired[:, :, 1, :], rows_next, rows_prev)
    half_width = width // 2
    coarse = low_rows[..., :half_width]
    if levels > 1:
        coarse = spatial_inplace(coarse, levels - 1)
    upper_rows = weave_axis(coarse, low_rows[..., half_width:], 2)
    bottom = weave_axis(high_rows[..., :half_width], high_rows[..., half_width:], 2)
    return jnp.stack([upper_rows, bottom], axis=2).reshape(frame_count, row_count, width)


def temporal(planes_in, levels):
    even_part = planes_in[0::2]
    odd_part = planes_in[1::2]
    odd_part = odd_part - 0.5 * (even_part + mirror_after(even_part, 0))
    even_part = even_part + 0.25 * (mirror_before(odd_part, 0) + odd_part)
    if levels > 1:
        even_part = temporal(even_part, levels - 1)
    return weave_axis(even_part, odd_part, 0)


def rows_next(values):
    arrived = shifted(values[:, :1], "row", -1)
    is_last = lax.axis_index("row") == lax.axis_size("row") - 1
    return jnp.concatenate([values[:, 1:], jnp.where(is_last, values[:, -1:], arrived)], axis=1)


def rows_prev(values):
    arrived = shifted(values[:, -1:], "row", 1)
    is_first = lax.axis_index("row") == 0
    return jnp.concatenate([jnp.where(is_first, values[:, :1], arrived), values[:, :-1]], axis=1)


def level_of(number, ceiling):
    depth_now = 1
    while number % 2 == 0 and depth_now <= ceiling:
        number = number // 2
        depth_now = depth_now + 1
    return depth_now


def space_table(levels):
    period = 2**levels
    band_table = np.zeros((period * period, 3 * levels + 1), np.float32)
    for row_pos in range(period):
        for col_pos in range(period):
            row_level = level_of(row_pos, levels)
            col_level = level_of(col_pos, levels)
            finest = min(row_level, col_level)
            if finest > levels:
                column = 3 * levels
            elif row_level == col_level:
                column = 3 * (finest - 1) + 2
            elif row_level == finest:
                column = 3 * (finest - 1)
            else:
                column = 3 * (finest - 1) + 1
            band_table[row_pos * period + col_pos, column] = 1.0
    return band_table


def time_table(levels):
    period = 2**levels
    band_table = np.zeros((period, levels + 1), np.float32)
    for number in range(period):
        band_table[number, level_of(number, levels) - 1] = 1.0
    return band_table


def band_sums(coeffs, first_frame, levels_s, levels_t):
    period = 2**levels_s
    frame_count, row_count, col_count = coeffs.shape
    square = coeffs * coeffs
    row_folded = square.reshape(frame_count, row_count // period, period, col_count).sum(axis=1)
    column_phase = np.arange(col_count) % period
    selector = jnp.asarray((column_phase[:, None] == np.arange(period)[None, :]).astype(np.float32))
    pattern = jnp.dot(row_folded, selector, precision=lax.Precision.HIGHEST)
    pattern = pattern.reshape(frame_count, period * period)
    per_frame = jnp.dot(
        pattern, jnp.asarray(space_table(levels_s), jnp.float32), precision=lax.Precision.HIGHEST
    )
    time_period = 2**levels_t
    position = (first_frame + jnp.arange(frame_count, dtype=jnp.int32)) % time_period
    onehot = (position[:, None] == jnp.arange(time_period, dtype=jnp.int32)[None, :]).astype(
        jnp.float32
    )
    frame_band = jnp.dot(
        onehot, jnp.asarray(time_table(levels_t), jnp.float32), precision=lax.Precision.HIGHEST
    )
    return jnp.dot(frame_band.T, per_frame, precision=lax.Precision.HIGHEST)


def band_means(totals, frames_all, rows_all, cols_all, levels_s, levels_t):
    space_share = space_table(levels_s).sum(0) / float((2**levels_s) ** 2)
    time_share = time_table(levels_t).sum(0) / float(2**levels_t)
    counts = (
        float(frames_all) * float(rows_all) * float(cols_all) * np.outer(time_share, space_share)
    )
    return totals / jnp.asarray(counts, jnp.float32)


def shards(footage):
    frames_dev = footage.shape[0]
    planes = spatial_inplace(footage, SLEVELS)
    temporal_out = temporal(
        lax.all_to_all(planes, "frame", split_axis=1, concat_axis=0, tiled=True), TLEVELS
    )
    coeffs = lax.all_to_all(temporal_out, "frame", split_axis=0, concat_axis=1, tiled=True)
    totals = band_sums(coeffs, lax.axis_index("frame") * frames_dev, SLEVELS, TLEVELS)
    totals = lax.psum(totals, ("frame", "row"))
    means = band_means(
        totals,
        frames_dev * lax.axis_size("frame"),
        coeffs.shape[1] * lax.axis_size("row"),
        coeffs.shape[2],
        SLEVELS,
        TLEVELS,
    )
    return (coeffs, means)


def solution(mesh):
    return jax.shard_map(
        shards,
        mesh=mesh,
        in_specs=(P("frame", "row", None),),
        out_specs=(P("frame", "row", None), P()),
        check_vma=False,
    )
```

profile of v0, /device:TPU:14, one launch (start us, length us, event | category | flops | bytes accessed | tf_op | source)
XLA Modules:
  0.0 669.8 jit_solution(6688530232217569210)
XLA Ops:
  0.6 31.4 %convolution_bitcast_fusion = f32[4,512,1024]{2,1,0:T(8,128)} fusion(f32[1024,1024,1]{1,0,2:T(8,128)} %constant.85, f32[4,512,1024]{2,1,0:T(8,128)} %param.8), kind=kOutput, calls=%fused_computation.26 | convolution fusion | flops 25769803776 | bytes 20971520 | tf_op jit(solution)/shard_map/dot_general | solution.py:83
  32.0 10.6 %reshape.40 = f32[4,256,2,1024]{3,2,1,0:T(2,128)} reshape(f32[4,512,1024]{2,1,0:T(8,128)} %convolution_bitcast_fusion) | data formatting | bytes 16777216 | tf_op jit(solution)/shard_map/reshape | solution.py:84
  42.6 10.7 %fusion.50 = (f32[4,256,1,1024]{3,2,1,0:T(1,128)}, f32[4,256,1,1024]{3,2,1,0:T(1,128)S(1)}) fusion(f32[4,256,2,1024]{3,2,1,0:T(2,128)} %reshape.40), kind=kLoop, calls=%fused_computation.109 | loop fusion | bytes 16777216 | tf_op jit(solution)/shard_map/slice | solution.py:85
  53.3 1.0 copy.80
  54.4 1.0 copy-done.2
  55.4 1.3 collective-permute-start
  57.4 2.5 slice.290
  59.9 0.9 broadcast_select_fusion.1
  60.8 7.3 %fusion.1 = f32[4,256,1024]{2,1,0:T(8,128)S(1)} fusion(f32[4,1,1024]{2,1,0:T(1,128)S(1)} %broadcast_select_fusion.1, f32[4,255,1024]{2,1,0:T(8,128)} %slice.290, f32[4,256,1,1024]{3,2,1,0:T(1,128)} %get-tuple-element.8, f32[4,256,1,1024]{3,2,1,0:T(1,128)} %copy-done.2), kind=kLoop, calls=%fused_computation.4 | loop fusion | flops 4194304 | bytes 16777216 | tf_op jit(solution)/shard_map/add | solution.py:54
  68.2 2.0 copy-done
  70.2 2.7 collective-permute-start.1
  74.3 6.8 %fusion.3 = f32[4,256,1024]{2,1,0:T(8,128)S(1)} fusion(f32[4,256,1024]{2,1,0:T(8,128)} %copy-done, f32[4,255,1024]{2,1,0:T(8,128)} %bitcast.99, f32[4,1,1024]{2,1,0:T(1,128)S(1)} %broadcast_select_fusion.3, f32[4,256,1,1024]{3,2,1,0:T(1,128)} %copy-done.2), kind=kLoop, calls=%fused_computation.7 | loop fusion | flops 4194304 | bytes 16777216 | tf_op jit(solution)/shard_map/add | solution.py:55
  81.1 1.6 collective-permute-start.2
  82.7 2.5 slice.296
  85.2 5.8 broadcast_multiply_fusion
  91.0 3.0 collective-permute-start.3
  94.9 1.6 fusion.8
  96.5 2.0 copy-done.5
  98.5 4.8 fusion.13
  103.4 2.5 reshape.41
  105.8 1.6 fusion.51
  107.6 1.6 collective-permute-start.4
  109.3 1.6 collective-permute-done.4
  111.3 2.1 collective-permute-start.5
  114.6 1.3 collective-permute-start.6
  115.9 2.5 pad_maximum_fusion.3
  118.4 5.4 copy.49
  124.4 3.3 collective-permute-start.7
  127.8 1.5 slice_bitcast_fusion.2
  130.6 1.1 fusion.53
  131.7 1.1 copy.62
  132.8 1.3 collective-permute-start.8
  134.1 1.1 slice_bitcast_fusion.4
  135.7 1.0 collective-permute-done.8
  137.1 1.0 slice.324
  138.1 2.9 collective-permute-start.9
  142.3 1.3 collective-permute-start.10
  144.7 1.7 collective-permute-done.10
  147.0 2.1 collective-permute-start.11
  151.8 1.2 stack_reshape.32
  153.0 1.1 pad_maximum_fusion.8
  154.1 1.3 copy.45
  155.5 1.4 pad_maximum_fusion.5
  156.8 2.4 copy.47
  159.2 3.9 stack_reshape.35
  163.1 4.2 pad_maximum_fusion.2
  167.3 5.5 copy.48
  172.9 8.8 %pad_maximum_fusion = f32[4,256,2,1024]{1,0,3,2:T(4,128)} fusion(f32[4,256,1,1024]{1,0,3,2:T(4,128)} %bitcast.112, f32[4,256,1,1024]{1,0,3,2:T(4,128)} %bitcast.113), kind=kLoop, calls=%fused_computation | loop fusion | flops 2097152 | bytes 16777216 | tf_op jit(solution)/shard_map/stack | solution.py:92
  181.7 11.4 %copy.50 = f32[4,256,2,1024]{3,0,2,1:T(4,128)} copy(f32[4,256,2,1024]{1,0,3,2:T(4,128)} %pad_maximum_fusion) | data formatting | bytes 16777216 | tf_op jit(solution)/shard_map/stack | solution.py:92
  193.1 189.2 %all_to_all.36 = f32[4,512,1024]{2,0,1:T(4,128)S(1)} all-to-all(f32[4,512,1024]{2,0,1:T(4,128)} %bitcast.104), channel_id=1, replica_groups=mesh['frame'=16,'row'=2] {'frame'}, dimensions={1} | all-to-all | bytes 16777216 | tf_op jit(solution)/shard_map/all_to_all | solution.py:189
  382.3 4.9 copy.51
  387.2 1.7 copy.52
  389.9 2.0 fusion.10
  392.4 2.0 fusion.12
  396.1 1.1 fusion.18
  399.8 1.7 pad_maximum_fusion.1
  401.4 4.2 copy.55
  405.7 6.7 all-to-all-start.1
  412.6 184.9 %all-to-all-done.1 = f32[64,32,1024]{2,1,0:T(8,128)} async-done(((f32[64,32,1024]{2,1,0:T(8,128)}), f32[64,32,1024]{2,1,0:T(8,128)}, u32[]{:S(2)}, u32[]{:S(2)}) %all-to-all-start.1) | async-done | bytes 8388640 | tf_op jit(solution)/shard_map/all_to_all | solution.py:191
  597.5 12.0 %mul.203 = f32[4,16,32,1024]{3,2,0,1:T(8,128)} multiply(f32[4,16,32,1024]{3,2,0,1:T(8,128)} %bitcast.39, f32[4,16,32,1024]{3,2,0,1:T(8,128)} %bitcast.39) | non-fusion elementwise | flops 2097152 | bytes 25165824 | tf_op jit(solution)/shard_map/mul | solution.py:156
  609.5 8.6 %copy.56 = f32[4,16,32,1024]{3,2,1,0:T(8,128)} copy(f32[4,16,32,1024]{3,2,0,1:T(8,128)} %bitcast.39) | data formatting | bytes 16777216 | tf_op jit(solution)/shard_map/all_to_all | solution.py:191
  618.1 4.1 copy.57
  622.2 3.9 reduce_sum.9
  626.8 41.9 %psum.7 = f32[4,10]{1,0:T(4,128)S(1)} all-reduce(f32[4,10]{1,0:T(4,128)S(1)} %fusion.56), channel_id=1, replica_groups=mesh['frame'=16,'row'=2] {'frame','row'}, use_global_device_ids=true, to_apply=%region_1.2 | all-reduce | flops 40 | bytes 320 | tf_op jit(solution)/shard_map/psum | solution.py:193
  (122 shorter events, 20.2 us)
Async XLA Ops:
  53.3 2.0 copy-start.2
  55.4 2.0 copy-start.4
  55.4 4.5 collective-permute-start
  68.2 2.0 copy-start
  70.2 3.2 collective-permute-start.1
  81.1 4.1 copy-start.1
  81.1 4.1 collective-permute-start.2
  91.0 3.9 collective-permute-start.3
  94.9 3.6 copy-start.14
  96.5 2.0 copy-start.5
  107.5 5.9 copy-start.7
  107.6 3.3 collective-permute-start.4
  111.3 2.9 collective-permute-start.5
  114.6 9.3 %collective-permute-start.6 = (f32[4,1,512]{2,1,0:T(1,128)S(1)}, f32[4,1,512]{2,1,0:T(1,128)S(1)}, u32[]{:S(2)}, u32[]{:S(2)}) collective-permute-start(f32[4,1,512]{2,1,0:T(1,128)S(1)} %slice.313), channel_id=1, source_target_pairs={{1,0},{3,2},{5,4},{7,6},{9,8},{11,10},{13,12},{15,14},{17,16},{19,... | collective-permute-start | bytes 24584 | tf_op jit(solution)/shard_map/ppermute | solution.py:21
  123.8 3.9 copy-start.6
  124.4 5.3 copy-start.15
  124.4 4.8 collective-permute-start.7
  129.7 7.2 %copy-start.9 = (f32[4,128,512]{2,1,0:T(8,128)}, f32[4,128,512]{2,1,0:T(8,128)S(1)}, u32[]{:S(2)}) copy-start(f32[4,128,512]{2,1,0:T(8,128)S(1)} %fusion.27) | copy-start | bytes 3145732
  132.8 3.8 collective-permute-start.8
  135.7 5.3 copy-start.12
  135.7 5.3 copy-start.13
  138.1 4.0 collective-permute-start.9
  141.6 2.0 copy-start.10
  142.3 4.1 collective-permute-start.10
  147.0 3.6 collective-permute-start.11
  150.9 2.1 copy-start.11
  159.2 3.9 copy-start.8
  405.7 6.7 copy-start.19
  405.7 191.8 %all-to-all-start.1 = ((f32[64,32,1024]{2,1,0:T(8,128)}), f32[64,32,1024]{2,1,0:T(8,128)}, u32[]{:S(2)}, u32[]{:S(2)}) async-start(f32[64,32,1024]{2,1,0:T(8,128)} %bitcast.102), calls=%async_computation.1 | async-start | bytes 16777216 | tf_op jit(solution)/shard_map/all_to_all | solution.py:191
  609.5 8.6 %copy-start.3 = (f32[4,16,32,1024]{3,2,0,1:T(8,128)S(1)}, f32[4,16,32,1024]{3,2,0,1:T(8,128)}, u32[]{:S(2)}) copy-start(f32[4,16,32,1024]{3,2,0,1:T(8,128)} %mul.203) | copy-start | bytes 25165828
  622.2 3.9 copy-start.17
  622.2 4.3 copy-start.16
  622.2 46.5 %copy-start.18 = (f32[4,10]{1,0:T(4,128)S(1)}, f32[4,10]{1,0:T(4,128)}, u32[]{:S(2)}) copy-start(f32[4,10]{1,0:T(4,128)} %constant.84) | copy-start | bytes 484
where the time goes:
time: 680 us; the launch traced here: 670 us
  blocking collectives  231 us (34%)
  waiting for transfers between devices  192 us (28%)
  local copies, waits for them, and re-layouts  105 us (15%)
  other arithmetic  70.7 us (10%)
  matrix products  37.5 us (6%)
  starting transfers between devices  31 us (5%)
    all_to_all x1, blocking collectives, shards(): lax.all_to_all(planes, 'frame', split_axis=1, concat_axis=0, tiled=True)  189 us
    all_to_all x1, waiting for transfers between devices, shards(): lax.all_to_all(temporal_out, 'frame', split_axis=0, concat_axis=1, tiled=...  185 us
    psum x1, blocking collectives, shards(): totals = lax.psum(totals, ('frame', 'row'))  41.9 us
    dot_general x3, matrix products, spatial_inplace(): jnp.dot(block, column_matrix(width), precision=lax.Precision.HIGHEST)  36.7 us
    another operation x15, local copies, waits for them, and re-layouts, weave_axis(): stacked = jnp.stack([even_part, odd_part], axis=along + 1)  27.3 us
    ppermute x12, starting transfers between devices, shifted(): return lax.ppermute(block, axis, route)  24.3 us
    another operation x3, local copies, waits for them, and re-layouts, spatial_inplace(): jnp.stack([upper_rows, bottom], axis=2)  14.1 us
  transfers between devices with their start and end apart: 13, of which 9 were waited for; matrix products, arithmetic and copies ran while one was open for 3% of the time, Pallas kernels for 0%

commit v1 on v0

v1 whole, which is shorter than its diff:
```python
import functools

import jax
import jax.numpy as jnp
import numpy as np
from jax import lax
from jax.experimental import pallas as pl
from jax.experimental.pallas import tpu as pltpu
from jax.sharding import PartitionSpec as P


SLEVELS = 3
TLEVELS = 3

LIFT_ALPHA = -1.586134342
LIFT_BETA = -0.05298011854
LIFT_GAMMA = 0.8829110762
LIFT_DELTA = 0.4435068522
LIFT_ZETA = 1.149604398
FACTORS = (LIFT_ALPHA, LIFT_BETA, LIFT_GAMMA, LIFT_DELTA)

LANES = 128
SUB = 8
HALO = 32
PAD = SUB
CHUNKS = 2
SPAN = 2 * 2**TLEVELS
KEPT = (0, 2, 3)


def level_of(number, ceiling):
    depth_now = 1
    while number % 2 == 0 and depth_now <= ceiling:
        number = number // 2
        depth_now = depth_now + 1
    return depth_now


def space_table(levels):
    period = 2**levels
    band_table = np.zeros((period * period, 3 * levels + 1), np.float32)
    for row_pos in range(period):
        for col_pos in range(period):
            row_level = level_of(row_pos, levels)
            col_level = level_of(col_pos, levels)
            finest = min(row_level, col_level)
            if finest > levels:
                column = 3 * levels
            elif row_level == col_level:
                column = 3 * (finest - 1) + 2
            elif row_level == finest:
                column = 3 * (finest - 1)
            else:
                column = 3 * (finest - 1) + 1
            band_table[row_pos * period + col_pos, column] = 1.0
    return band_table


def time_table(levels):
    period = 2**levels
    band_table = np.zeros((period, levels + 1), np.float32)
    for number in range(period):
        band_table[number, level_of(number, levels) - 1] = 1.0
    return band_table


def band_means(totals, frames_all, rows_all, cols_all, levels_s, levels_t):
    space_share = space_table(levels_s).sum(0) / float((2**levels_s) ** 2)
    time_share = time_table(levels_t).sum(0) / float(2**levels_t)
    counts = (
        float(frames_all) * float(rows_all) * float(cols_all) * np.outer(time_share, space_share)
    )
    return totals / jnp.asarray(counts, jnp.float32)


def lift_rows(buf, count):
    groups = count // SUB

    def step(odd, factor):
        target, near, far = (1, 0, 2) if odd else (0, -1, 1)

        def body(k, carry):
            top = PAD + 2 * SUB * k
            at = pl.ds(top + target, SUB, stride=2)
            for j in range(buf.shape[0]):
                buf[j, at, :] = buf[j, at, :] + factor * (
                    buf[j, pl.ds(top + near, SUB, stride=2), :]
                    + buf[j, pl.ds(top + far, SUB, stride=2), :]
                )
            return carry

        lax.fori_loop(0, groups, body, 0, unroll=2)

    step(True, LIFT_ALPHA)
    step(False, LIFT_BETA)
    step(True, LIFT_GAMMA)
    step(False, LIFT_DELTA)


def filter_taps():
    size = 8 * len(FACTORS)
    lifted = np.eye(size)
    for count, factor in enumerate(FACTORS):
        for n in range(1 - count % 2, size - 1, 2):
            lifted[n] += factor * (lifted[n - 1] + lifted[n + 1])
    middle = size // 2
    reach = len(FACTORS) + 1
    low = [lifted[middle, middle + k] * LIFT_ZETA for k in range(reach)]
    high = [lifted[middle + 1, middle + 1 + k] / LIFT_ZETA for k in range(reach)]
    return low, high


def lift_cols(buf, first, rows, stride):
    blocks = buf.shape[0]
    lane = lax.broadcasted_iota(jnp.int32, (SUB, LANES), 1)
    sub = lax.broadcasted_iota(jnp.int32, (SUB, LANES), 0)
    phase = lane % (2 * stride)
    low, high = filter_taps()
    reach = len(low)
    row_scale = jnp.where(sub % 2 == 0, jnp.float32(LIFT_ZETA), jnp.float32(1.0 / LIFT_ZETA))
    taps = [
        row_scale
        * jnp.where(
            phase == 0, jnp.float32(low[k]), jnp.where(phase == stride, jnp.float32(high[k]), 0.0)
        )
        for k in range(reach)
    ]
    shifts = [k * stride for k in range(reach)]
    head = [lane < shift for shift in shifts]
    tail = [lane >= LANES - shift for shift in shifts]

    def mirrored(x, source):
        return jnp.take_along_axis(x, source % LANES, axis=1)

    def body(i, carry):
        at = pl.ds(first + SUB * i, SUB)
        v = [buf[j, at, :] for j in range(blocks)]
        sums = [taps[0] * x for x in v]
        for k in range(1, reach):
            shift = shifts[k]
            up = [pltpu.roll(x, shift, 1) for x in v]
            down = [pltpu.roll(x, LANES - shift, 1) for x in v]
            left = mirrored(v[0], shift - lane)
            right = mirrored(v[-1], 2 * LANES - 2 * stride - shift - lane)
            for j in range(blocks):
                before = jnp.where(head[k], left if j == 0 else up[j - 1], up[j])
                after = jnp.where(tail[k], right if j == blocks - 1 else down[j + 1], down[j])
                sums[j] = sums[j] + taps[k] * (before + after)
        for j in range(blocks):
            buf[j, at, :] = sums[j]
        return carry

    lax.fori_loop(0, rows // SUB, body, 0, unroll=6)


def spatial_frame(x_ref, top_ref, bottom_ref, bufs):
    rows, width = x_ref.shape
    row_index = lax.axis_index("row")
    is_first = row_index == 0
    is_last = row_index == lax.axis_size("row") - 1
    first = PAD + HALO
    end = first + rows
    b = bufs[0]
    for j in range(width // LANES):
        c = slice(j * LANES, (j + 1) * LANES)
        b[j, first:end, :] = x_ref[:, c]
        b[j, PAD:first, :] = top_ref[:, c]
        b[j, end : end + HALO, :] = bottom_ref[:, c]

    @pl.when(is_first)
    def _():
        for j in range(1, HALO):
            b[:, first - j : first - j + 1, :] = b[:, first + j : first + j + 1, :]

    total = rows + 2 * HALO
    for level in range(SLEVELS):
        b = bufs[level]
        stride = 2**level
        count = total // stride
        inner = HALO // stride
        stop = PAD + inner + rows // stride

        @pl.when(is_last)
        def _(b=b, stop=stop, level=level, inner=inner):
            for j in range(inner - 1 if level == 0 else inner * 5 // 8):
                b[:, stop + j : stop + j + 1, :] = b[:, stop - 2 - j : stop - 1 - j, :]

        lift_rows(b, count // 2)
        lift_cols(b, PAD, count, stride)
        if level + 1 < SLEVELS:
            low = bufs[level + 1]

            def body(k, carry, b=b, low=low):
                for j in range(b.shape[0]):
                    low[j, pl.ds(PAD + SUB * k, SUB), :] = b[
                        j, pl.ds(PAD + 2 * SUB * k, SUB, stride=2), :
                    ]
                return carry

            lax.fori_loop(0, count // 2 // SUB, body, 0)
    lane = lax.broadcasted_iota(jnp.int32, (SUB, LANES), 1)
    for level in reversed(range(SLEVELS - 1)):
        b, low = bufs[level], bufs[level + 1]
        stride = 2 ** (level + 1)
        keep = lane % stride == 0

        def body(k, carry, b=b, low=low, keep=keep, stride=stride):
            at = pl.ds(PAD + HALO // (stride // 2) + 2 * SUB * k, SUB, stride=2)
            inner = pl.ds(PAD + HALO // stride + SUB * k, SUB)
            for j in range(b.shape[0]):
                b[j, at, :] = jnp.where(keep, low[j, inner, :], b[j, at, :])
            return carry

        lax.fori_loop(0, rows // stride // SUB, body, 0)


def member(group):
    return lax.axis_index("frame") % group


def space_first_kernel(group, x_ref, top_ref, bottom_ref, *refs):
    pieces, plane, bufs = refs[:group], refs[group], refs[group + 1 :]
    spatial_frame(x_ref.at[0], top_ref.at[0], bottom_ref.at[0], bufs)
    rows = x_ref.shape[1]
    first = PAD + HALO
    me = member(group)
    part = rows // group
    for d in range(group):
        start = pl.multiple_of(first + (me ^ d) * part, SUB)
        for j in range(bufs[0].shape[0]):
            c = slice(j * LANES, (j + 1) * LANES)
            pieces[d][0, :, c] = bufs[0][j, pl.ds(start, part), :]
    for j in range(bufs[0].shape[0]):
        plane[:, j * LANES : (j + 1) * LANES] = bufs[0][j, first : first + rows, :]


def space_rest_kernel(group, x_ref, top_ref, bottom_ref, plane_ref, *refs):
    count = group * CHUNKS
    pieces, out, held, bufs = refs[:count], refs[count], refs[count + 1], refs[count + 2 :]
    spatial_frame(x_ref.at[0], top_ref.at[0], bottom_ref.at[0], bufs)
    rows = x_ref.shape[1]
    first = PAD + HALO
    me = member(group)
    part = rows // group
    piece = part // CHUNKS
    for d in range(group):
        for c in range(CHUNKS):
            start = pl.multiple_of(first + (me ^ d) * part + c * piece, SUB)
            for j in range(bufs[0].shape[0]):
                at = slice(j * LANES, (j + 1) * LANES)
                pieces[d * CHUNKS + c][0, :, at] = bufs[0][j, pl.ds(start, piece), :]

    @pl.when(pl.program_id(0) == 0)
    def _():
        for j in range(bufs[0].shape[0]):
            at = slice(j * LANES, (j + 1) * LANES)
            held[j] = bufs[0][j, first : first + rows, :] - 0.5 * plane_ref[:, at]

    @pl.when(pl.program_id(0) == 1)
    def _():
        for j in range(bufs[0].shape[0]):
            at = slice(j * LANES, (j + 1) * LANES)
            out[0, :, at] = held[j] - 0.5 * bufs[0][j, first : first + rows, :]


def space_scratch(rows, width):
    total = rows + 2 * HALO
    return [
        pltpu.VMEM((width // LANES, total // 2**level + 2 * PAD, LANES), jnp.float32)
        for level in range(SLEVELS)
    ]


def space(footage, top, bottom, group):
    frames, rows, width = footage.shape
    part = rows // group
    piece = part // CHUNKS
    f32 = jnp.float32

    def ins(shift):
        return [
            pl.BlockSpec((1, rows, width), lambda g: (g + shift, 0, 0)),
            pl.BlockSpec((1, HALO, width), lambda g: (g + shift, 0, 0)),
            pl.BlockSpec((1, HALO, width), lambda g: (g + shift, 0, 0)),
        ]

    def cost(count):
        return pl.CostEstimate(
            flops=count * rows * width * 400, bytes_accessed=count * rows * width * 8, transcendentals=0
        )

    outs = pl.pallas_call(
        functools.partial(space_first_kernel, group),
        grid=(1,),
        in_specs=ins(0),
        out_specs=[pl.BlockSpec((1, part, width), lambda g: (0, 0, 0))] * group
        + [pl.BlockSpec((rows, width), lambda g: (0, 0))],
        out_shape=[jax.ShapeDtypeStruct((1, part, width), f32)] * group
        + [jax.ShapeDtypeStruct((rows, width), f32)],
        scratch_shapes=space_scratch(rows, width),
        cost_estimate=cost(1),
        name="space_first",
    )(footage, top, bottom)
    firsts, plane = outs[:group], outs[group]
    outs = pl.pallas_call(
        functools.partial(space_rest_kernel, group),
        grid=(frames - 1,),
        in_specs=ins(1) + [pl.BlockSpec((rows, width), lambda g: (0, 0))],
        out_specs=[pl.BlockSpec((1, piece, width), lambda g: (g, 0, 0))] * (group * CHUNKS)
        + [pl.BlockSpec((1, rows, width), lambda g: (1, 0, 0))],
        out_shape=[jax.ShapeDtypeStruct((frames - 1, piece, width), f32)] * (group * CHUNKS)
        + [jax.ShapeDtypeStruct((frames, rows, width), f32)],
        scratch_shapes=[pltpu.VMEM((width // LANES, rows, LANES), f32)] + space_scratch(rows, width),
        cost_estimate=cost(frames - 1),
        name="space_rest",
    )(footage, top, bottom, plane)
    rest = [[outs[d * CHUNKS + c] for d in range(group)] for c in range(CHUNKS)]
    return firsts, rest, outs[-1]


WIDE = 2 * LANES
BLOCK_ROWS = 16


def gather_span(group, firsts, rest, span):
    me = member(group)
    for d in range(group):
        base = (me ^ d) * (SPAN // group)
        span[base] = firsts[d][0]
        for f in range(SPAN // group - 1):
            span[base + 1 + f] = rest[d][f]


def each_tile(rows, width, body):
    tiles = width // WIDE

    def step(k, carry):
        r = pl.multiple_of((k // tiles) * SUB, SUB)
        c = pl.multiple_of((k % tiles) * WIDE, WIDE)
        body(pl.ds(r, SUB), pl.ds(c, WIDE))
        return carry

    lax.fori_loop(0, rows // SUB * tiles, step, 0)


def partial_levels(x):
    o = {n: x[n] - 0.5 * (x[n - 1] + x[n + 1]) for n in range(1, SPAN - 1, 2)}
    o[15] = x[15] - 0.5 * x[14]
    low = {n: x[n] + 0.25 * (o[n - 1] + o[n + 1]) for n in range(2, SPAN, 2)}
    low[0] = x[0] + 0.25 * o[1]
    p = {n: low[n] - 0.5 * (low[n - 2] + low[n + 2]) for n in (2, 6, 10)}
    p[14] = low[14] - 0.5 * low[12]
    m = {n: low[n] + 0.25 * (p[n - 2] + p[n + 2]) for n in (8, 12)}
    m[0] = low[0] + 0.25 * p[2]
    q12 = m[12] - 0.5 * m[8]
    to_right = (o[15], p[14], q12)
    to_left = (x[0], low[0], m[0])
    return to_right, to_left


def full_levels(x, left, right, is_first, is_last):
    a0, b0, c0 = left
    x16, low16, m16 = right
    o = {n: x[n] - 0.5 * (x[n - 1] + x[n + 1]) for n in range(1, SPAN - 1, 2)}
    o[15] = x[15] - 0.5 * (x[14] + jnp.where(is_last, x[14], x16))
    before = jnp.where(is_first, o[1], a0 - 0.5 * x[0])
    low = {n: x[n] + 0.25 * (o[n - 1] + o[n + 1]) for n in range(2, SPAN, 2)}
    low[0] = x[0] + 0.25 * (before + o[1])
    p = {n: low[n] - 0.5 * (low[n - 2] + low[n + 2]) for n in (2, 6, 10)}
    p[14] = low[14] - 0.5 * (low[12] + jnp.where(is_last, low[12], low16 + 0.25 * o[15]))
    before = jnp.where(is_first, p[2], b0 - 0.125 * x[0] - 0.5 * low[0])
    m = {n: low[n] + 0.25 * (p[n - 2] + p[n + 2]) for n in (4, 8, 12)}
    m[0] = low[0] + 0.25 * (before + p[2])
    q4 = m[4] - 0.5 * (m[0] + m[8])
    after = jnp.where(is_last, m[8], m16 + 0.21875 * o[15] + 0.25 * p[14])
    q12 = m[12] - 0.5 * (m[8] + after)
    before = jnp.where(is_first, q4, c0 - 0.03125 * x[0] - 0.125 * low[0] - 0.5 * m[0])
    y = dict(o)
    y.update(p)
    y[4] = q4
    y[12] = q12
    y[0] = m[0] + 0.25 * (before + q4)
    y[8] = m[8] + 0.25 * (q4 + q12)
    return [y[n] for n in range(SPAN)]


def edges_kernel(group, *refs):
    firsts, rest = refs[:group], refs[group : 2 * group]
    to_right, to_left, span = refs[2 * group :]
    gather_span(group, firsts, rest, span)
    _, rows, width = span.shape

    def body(r, c):
        right, left = partial_levels([span[n, r, c] for n in range(SPAN)])
        for k in range(TLEVELS):
            to_right[k, r, c] = right[k]
            to_left[k, r, c] = left[k]

    each_tile(rows, width, body)


def time_kernel(group, *refs):
    firsts, rest = refs[:group], refs[group : 2 * group]
    left, right = refs[2 * group : 2 * group + 2]
    pieces = refs[2 * group + 2 : 3 * group + 2]
    power, span = refs[3 * group + 2 :]
    gather_span(group, firsts, rest, span)
    _, rows, width = span.shape
    spot = lax.axis_index("frame") // group
    is_first = spot == 0
    is_last = spot == lax.axis_size("frame") // group - 1

    @pl.when(pl.program_id(0) == 0)
    def _():
        power[...] = jnp.zeros_like(power)

    def body(r, c):
        y = full_levels(
            [span[n, r, c] for n in range(SPAN)],
            [left[k, r, c] for k in range(TLEVELS)],
            [right[k, r, c] for k in range(TLEVELS)],
            is_first,
            is_last,
        )
        sums = [None] * (TLEVELS + 1)
        for n in range(SPAN):
            t = level_of(n % 2**TLEVELS, TLEVELS) - 1
            square = y[n] * y[n]
            sums[t] = square if sums[t] is None else sums[t] + square
            span[n, r, c] = y[n]
        for t in range(TLEVELS + 1):
            power[t, :, c] = power[t, :, c] + sums[t]

    each_tile(rows, width, body)
    me = member(group)
    for d in range(group):
        base = (me ^ d) * (SPAN // group)
        for k, f in enumerate(KEPT):
            pieces[d][k] = span[base + f]


def span_specs(group, chunk, piece, width):
    steps = piece // BLOCK_ROWS
    return [
        pl.BlockSpec((1, BLOCK_ROWS, width), lambda i: (0, chunk * steps + i, 0))
    ] * group + [pl.BlockSpec((SPAN // group - 1, BLOCK_ROWS, width), lambda i: (0, i, 0))] * group


def span_cost(piece, width, flops, frames):
    return pl.CostEstimate(
        flops=piece * width * flops, bytes_accessed=piece * width * 4 * frames, transcendentals=0
    )


def edges(group, chunk, firsts, rest):
    _, piece, width = rest[0].shape
    spec = pl.BlockSpec((TLEVELS, BLOCK_ROWS, width), lambda i: (0, i, 0))
    shape = jax.ShapeDtypeStruct((TLEVELS, piece, width), jnp.float32)
    return pl.pallas_call(
        functools.partial(edges_kernel, group),
        grid=(piece // BLOCK_ROWS,),
        in_specs=span_specs(group, chunk, piece, width),
        out_specs=[spec, spec],
        out_shape=[shape, shape],
        scratch_shapes=[pltpu.VMEM((SPAN, BLOCK_ROWS, width), jnp.float32)],
        cost_estimate=span_cost(piece, width, 2000, SPAN + 6),
    )(*firsts, *rest)


def finish_time(group, chunk, firsts, rest, left, right):
    _, piece, width = rest[0].shape
    kept = len(KEPT)
    halo = pl.BlockSpec((TLEVELS, BLOCK_ROWS, width), lambda i: (0, i, 0))
    outs = pl.pallas_call(
        functools.partial(time_kernel, group),
        grid=(piece // BLOCK_ROWS,),
        in_specs=span_specs(group, chunk, piece, width) + [halo, halo],
        out_specs=[pl.BlockSpec((kept, BLOCK_ROWS, width), lambda i: (0, i, 0))] * group
        + [pl.BlockSpec((TLEVELS + 1, SUB, width), lambda i: (0, 0, 0))],
        out_shape=[jax.ShapeDtypeStruct((kept, piece, width), jnp.float32)] * group
        + [jax.ShapeDtypeStruct((TLEVELS + 1, SUB, width), jnp.float32)],
        scratch_shapes=[pltpu.VMEM((SPAN, BLOCK_ROWS, width), jnp.float32)],
        cost_estimate=span_cost(piece, width, 2000, 2 * SPAN + 6),
    )(*firsts, *rest, left, right)
    return outs[:group], outs[group]


def place_kernel(group, chunk, *refs):
    pieces, out, sems = refs[:group], refs[group + 1], refs[group + 2]
    k = pl.program_id(0)
    frame = jnp.where(k == 0, KEPT[0], k + 1)
    _, rows, _ = pieces[0].shape
    part = rows * CHUNKS
    me = member(group)
    copies = []
    for d in range(group):
        start = pl.multiple_of((me ^ d) * part + chunk * rows, SUB)
        copies.append(
            pltpu.make_async_copy(pieces[d].at[0], out.at[frame, pl.ds(start, rows)], sems.at[d])
        )
    for copy in copies:
        copy.start()
    for copy in copies:
        copy.wait()


def place(group, chunk, pieces, coeffs):
    kept, piece, width = pieces[0].shape
    return pl.pallas_call(
        functools.partial(place_kernel, group, chunk),
        grid=(kept,),
        in_specs=[pl.BlockSpec((1, piece, width), lambda k: (k, 0, 0))] * group
        + [pl.BlockSpec(memory_space=pl.ANY)],
        out_specs=pl.BlockSpec(memory_space=pl.ANY),
        out_shape=jax.ShapeDtypeStruct(coeffs.shape, coeffs.dtype),
        input_output_aliases={group: 0},
        scratch_shapes=[pltpu.SemaphoreType.DMA((group,))],
        cost_estimate=span_cost(piece, width, 100, 2 * kept * group),
    )(*pieces, coeffs)


def swap(blocks, group):
    devices = range(lax.axis_size("frame"))
    out = [blocks[0]]
    for d in range(1, group):
        out.append(lax.ppermute(blocks[d], "frame", [(i, i ^ d) for i in devices]))
    return out


def shifted(block, axis, distance):
    devices = range(lax.axis_size(axis))
    route = [(i - distance, i) for i in devices if i - distance in devices]
    return lax.ppermute(block, axis, route)


def doubled(total, axis, bit):
    devices = range(lax.axis_size(axis))
    return total + lax.ppermute(total, axis, [(i, i ^ bit) for i in devices])


def total_of_all(totals, group):
    sizes = [lax.axis_size("row"), lax.axis_size("frame")]
    if any(size & (size - 1) for size in sizes):
        return lax.psum(totals, ("frame", "row"))
    bit = 1
    while bit < sizes[0]:
        totals = doubled(totals, "row", bit)
        bit *= 2
    bit = group
    while bit < sizes[1]:
        totals = doubled(totals, "frame", bit)
        bit *= 2
    parts = swap([totals] * group, group)
    while len(parts) > 1:
        parts = [parts[k] + parts[k + 1] for k in range(0, len(parts), 2)]
    return parts[0]


def shards(footage):
    frames, rows, width = footage.shape
    group = SPAN // frames
    top = shifted(footage[:, rows - HALO :], "row", 1)
    bottom = shifted(footage[:, :HALO], "row", -1)
    firsts, rest, coeffs = space(footage, top, bottom, group)
    firsts = swap(firsts, group)
    rest = [swap(r, group) for r in rest]
    power = None
    back = []
    for c in range(CHUNKS):
        to_right, to_left = edges(group, c, firsts, rest[c])
        left = shifted(to_right, "frame", group)
        right = shifted(to_left, "frame", -group)
        pieces, part_power = finish_time(group, c, firsts, rest[c], left, right)
        back.append(swap(pieces, group))
        power = part_power if power is None else power + part_power
    period = 2**SLEVELS
    column_phase = np.arange(width) % period
    selector = jnp.asarray((column_phase[:, None] == np.arange(period)[None, :]).astype(np.float32))
    pattern = jnp.dot(
        power.reshape((TLEVELS + 1) * SUB, width), selector, precision=lax.Precision.HIGHEST
    ).reshape(TLEVELS + 1, SUB * period)
    totals = jnp.dot(
        pattern, jnp.asarray(space_table(SLEVELS), jnp.float32), precision=lax.Precision.HIGHEST
    )
    totals = total_of_all(totals, group)
    for c in range(CHUNKS):
        coeffs = place(group, c, back[c], coeffs)
    means = band_means(
        totals,
        frames * lax.axis_size("frame"),
        rows * lax.axis_size("row"),
        width,
        SLEVELS,
        TLEVELS,
    )
    return (coeffs, means)


def solution(mesh):
    return jax.shard_map(
        shards,
        mesh=mesh,
        in_specs=(P("frame", "row", None),),
        out_specs=(P("frame", "row", None), P()),
        check_vma=False,
    )
```

time: 680 us -> 298 us (0.44)
  blocking collectives: 231 us -> 0 us
  Pallas kernels: 0 us -> 106 us
  local copies, waits for them, and re-layouts: 105 us -> 5.15 us
  other arithmetic: 70.7 us -> 0.59 us
  waiting for transfers between devices: 192 us -> 145 us
  matrix products: 37.5 us -> 1.5 us
    all_to_all x1 -> x0, blocking collectives: 189 us -> none  [shards(): lax.all_to_all(planes, 'frame', split_axis=1, concat_axis=0, tiled=True)]
    all_to_all x1 -> x0, waiting for transfers between devices: 185 us -> none  [shards(): lax.all_to_all(temporal_out, 'frame', split_axis=0, concat_axis=1, tiled=...]
    ppermute x0 -> x21, waiting for transfers between devices: none -> 132 us  [the longest x18 126 us: swap(): out.append(lax.ppermute(blocks[d], 'frame', [(i, i ^ d) for i in devices]))]
    pallas_call x0 -> x8, Pallas kernels: none -> 106 us  [the longest x1 54.6 us: space(): pl.pallas_call(functools.partial(space_rest_kernel, group), grid=(frames...]
    psum x1 -> x0, blocking collectives: 41.9 us -> none  [shards(): totals = lax.psum(totals, ('frame', 'row'))]
    another operation x18 -> x0, local copies, waits for them, and re-layouts: 41.4 us -> none  [the longest x15 27.3 us: weave_axis(): stacked = jnp.stack([even_part, odd_part], axis=along + 1)]
    dot_general x7 -> x2, matrix products: 37.5 us -> 1.5 us  [the longest x1 1.36 us: shards(): jnp.dot(power.reshape((TLEVELS + 1) * SUB, width), selector, precision=la...]
    slice x35 -> x1, local copies, waits for them, and re-layouts: 22.9 us -> 1.31 us  [shards(): bottom = shifted(footage[:, :HALO], 'row', -1)]
  transfers between devices with their start and end apart: 13 -> 27, of which waited for: 9 -> 15; matrix products, arithmetic and copies ran while one was open for 3% -> 1% of each run, Pallas kernels for 0% -> 28%
where the time goes in v1:
time: 298 us; the launch traced here: 293 us
  waiting for transfers between devices  145 us (49%)
  Pallas kernels  106 us (36%)
  starting transfers between devices  34.3 us (12%)
  local copies, waits for them, and re-layouts  5.15 us (2%)
    ppermute x18, waiting for transfers between devices, swap(): out.append(lax.ppermute(blocks[d], 'frame', [(i, i ^ d) for i in devices]))  126 us
    pallas_call x1, Pallas kernels, space(): pl.pallas_call(functools.partial(space_rest_kernel, group), grid=(frames...  54.6 us
    pallas_call x1, Pallas kernels, space(): pl.pallas_call(functools.partial(space_first_kernel, group), grid=(1,), i...  20 us
    ppermute x18, starting transfers between devices, swap(): out.append(lax.ppermute(blocks[d], 'frame', [(i, i ^ d) for i in devices]))  17.9 us
    ppermute x6, starting transfers between devices, shifted(): return lax.ppermute(block, axis, route)  15 us
    ppermute x6, waiting for transfers between devices, shifted(): return lax.ppermute(block, axis, route)  12.5 us
    pallas_call x2, Pallas kernels, finish_time(): pl.pallas_call(functools.partial(time_kernel, group), grid=(piece // BLOC...  12.4 us
    pallas_call x2, Pallas kernels, edges(): pl.pallas_call(functools.partial(edges_kernel, group), grid=(piece // BLO...  9.65 us
  transfers between devices with their start and end apart: 27, of which 15 were waited for; matrix products, arithmetic and copies ran while one was open for 1% of the time, Pallas kernels for 28%

profile of v1, /device:TPU:14, one launch (start us, length us, event | category | flops | bytes accessed | tf_op | source)
XLA Modules:
  0.0 293.5 jit_solution(16505777430974001717)
XLA Ops:
  0.6 1.3 fusion.1
  1.9 1.8 collective-permute-start
  3.7 1.3 collective-permute-start.1
  5.0 0.2 collective-permute-done.top_ref
  5.2 2.3 collective-permute-done.1.bottom_ref
  7.5 0.8 copy-done.6
  8.3 20.0 %space_first.1 = (f32[1,128,1024]{2,1,0:T(8,128)}, f32[1,128,1024]{2,1,0:T(8,128)}, f32[1,128,1024]{2,1,0:T(8,128)}, f32[1,128,1024]{2,1,0:T(8,128)}, f32[512,1024]{1,0:T(8,128)}) custom-call(f32[4,512,1024]{2,1,0:T(8,128)} %x_ref.3, f32[4,32,1024]{2,1,0:T(8,128)} %copy-done.5, f32[4,32,1024]{2,1,0:T(8,128)} %copy-done.6), custom_call_target="tpu_custom_call" | custom-call | flops 209715200 | bytes 4194304 | tf_op jit(solution)/shard_map/space_first/pallas_call | solution.py:292
  28.3 0.5 collective-permute-start.2
  28.9 54.6 %space_rest.1 = (f32[3,64,1024]{2,1,0:T(8,128)}, f32[3,64,1024]{2,1,0:T(8,128)}, f32[3,64,1024]{2,1,0:T(8,128)}, f32[3,64,1024]{2,1,0:T(8,128)}, f32[3,64,1024]{...) custom-call(f32[4,512,1024]{2,1,0:T(8,128)} %x_ref.3, ...), custom_call_target="tpu_custom_call" | custom-call | flops 629145600 | bytes 12582912 | tf_op jit(solution)/shard_map/space_rest/pallas_call | solution.py:305
  83.5 1.6 collective-permute-start.13
  85.0 0.5 collective-permute-start.3
  85.5 1.5 collective-permute-start.4
  87.0 0.5 collective-permute-start.14
  87.5 2.4 collective-permute-start.15
  90.0 9.8 %collective-permute-done.3.refs_2_ = f32[1,128,1024]{2,1,0:T(8,128)S(1)} collective-permute-done((f32[1,128,1024]{2,1,0:T(8,128)S(1)}, f32[1,128,1024]{2,1,0:T(8,128)S(1)}, u32[]{:S(2)}, u32[]{:S(2)}) %collective-permute-start.3) | collective-permute-done | bytes 524320 | tf_op jit(solution)/shard_map/ppermute | solution.py:526
  99.8 0.5 collective-permute-start.5
  100.4 15.1 %collective-permute-done.4.refs_3_ = f32[1,128,1024]{2,1,0:T(8,128)S(1)} collective-permute-done((f32[1,128,1024]{2,1,0:T(8,128)}, f32[1,128,1024]{2,1,0:T(8,128)S(1)}, u32[]{:S(2)}, u32[]{:S(2)}) %collective-permute-start.4) | collective-permute-done | bytes 524320 | tf_op jit(solution)/shard_map/ppermute | solution.py:526
  115.4 1.5 collective-permute-start.6
  117.0 0.0 collective-permute-done.13.refs_5_
  117.0 1.4 collective-permute-start.7
  118.4 26.5 %collective-permute-done.14.refs_6_ = f32[3,64,1024]{2,1,0:T(8,128)} collective-permute-done((f32[3,64,1024]{2,1,0:T(8,128)}, f32[3,64,1024]{2,1,0:T(8,128)}, u32[]{:S(2)}, u32[]{:S(2)}) %collective-permute-start.14) | collective-permute-done | bytes 786464 | tf_op jit(solution)/shard_map/ppermute | solution.py:526
  144.9 0.0 collective-permute-done.15.refs_7_
  144.9 4.8 %shard_map.61 = (f32[3,64,1024]{2,1,0:T(8,128)}, f32[3,64,1024]{2,1,0:T(8,128)}) custom-call(f32[1,128,1024]{2,1,0:T(8,128)} %get-tuple-element.30.refs_0_, f32[1,128,1024]{2,1,0:T(8,128)} %copy-done, f32[1,128,1024]{2,1,0:T(8,128)} %copy-done.1, f32[1,128,1024]{2,1,0:T(8,128)} %copy-done.2, f32[3,64,1024]{2,1,0:T(8,128)} %get-tuple-element.45.refs_4_, ...), custom_call_target="tpu_custom_call" | custom-call | flops 131072000 | bytes 5767168 | tf_op jit(solution)/shard_map/pallas_call | solution.py:459
  149.7 3.5 %collective-permute-start.16 = (f32[3,64,1024]{2,1,0:T(8,128)}, f32[3,64,1024]{2,1,0:T(8,128)S(1)}, u32[]{:S(2)}, u32[]{:S(2)}) collective-permute-start(f32[3,64,1024]{2,1,0:T(8,128)} %get-tuple-element.49), channel_id=1, source_target_pairs={{0,8},{2,10},{4,12},{6,14},{8,16},{10,18},{12,20},{14,22},{16,24},... | collective-permute-start | bytes 2359304 | tf_op jit(solution)/shard_map/ppermute | solution.py:533
  153.2 2.4 collective-permute-start.17
  155.6 0.0 collective-permute-done.5.refs_5_
  155.6 21.7 %collective-permute-done.6.refs_6_ = f32[3,64,1024]{2,1,0:T(8,128)} collective-permute-done((f32[3,64,1024]{2,1,0:T(8,128)}, f32[3,64,1024]{2,1,0:T(8,128)}, u32[]{:S(2)}, u32[]{:S(2)}) %collective-permute-start.6) | collective-permute-done | bytes 786464 | tf_op jit(solution)/shard_map/ppermute | solution.py:526
  177.4 4.8 %shard_map.59 = (f32[3,64,1024]{2,1,0:T(8,128)}, f32[3,64,1024]{2,1,0:T(8,128)}) custom-call(f32[1,128,1024]{2,1,0:T(8,128)} %get-tuple-element.30.refs_0_, f32[1,128,1024]{2,1,0:T(8,128)} %copy-done, f32[1,128,1024]{2,1,0:T(8,128)} %copy-done.1, f32[1,128,1024]{2,1,0:T(8,128)} %copy-done.2, f32[3,64,1024]{2,1,0:T(8,128)} %get-tuple-element.35.refs_4_, ...), custom_call_target="tpu_custom_call" | custom-call | flops 131072000 | bytes 5767168 | tf_op jit(solution)/shard_map/pallas_call | solution.py:459
  182.2 0.0 copy-start.15
  182.2 0.0 copy-start.16
  182.2 3.6 %collective-permute-start.8 = (f32[3,64,1024]{2,1,0:T(8,128)}, f32[3,64,1024]{2,1,0:T(8,128)S(1)}, u32[]{:S(2)}, u32[]{:S(2)}) collective-permute-start(f32[3,64,1024]{2,1,0:T(8,128)} %get-tuple-element.39), channel_id=1, source_target_pairs={{0,8},{2,10},{4,12},{6,14},{8,16},{10,18},{12,20},{14,22},{16,24},... | collective-permute-start | bytes 2359304 | tf_op jit(solution)/shard_map/ppermute | solution.py:533
  185.9 2.4 collective-permute-start.9
  188.3 0.9 copy-done.12
  189.2 6.2 %shard_map.62 = (f32[3,64,1024]{2,1,0:T(8,128)}, f32[3,64,1024]{2,1,0:T(8,128)}, f32[3,64,1024]{2,1,0:T(8,128)}, f32[3,64,1024]{2,1,0:T(8,128)}, f32[4,8,1024]{2,1,0:T(8,128)}) custom-call(f32[1,128,1024]{2,1,0:T(8,128)} %get-tuple-element.30.refs_0_, f32[1,128,1024]{2,1,0:T(8,128)} %copy-done, f32[1,128,1024]{2,1,0:T(8,128)} %copy-done.1, ...), custom_call_target="tpu_custom_call" | custom-call | flops 131072000 | bytes 9961472 | tf_op jit(solution)/shard_map/pallas_call | solution.py:474
  195.4 0.6 collective-permute-start.18
  196.0 6.8 %collective-permute-done.8.refs_8_ = f32[3,64,1024]{2,1,0:T(8,128)S(1)} collective-permute-done((f32[3,64,1024]{2,1,0:T(8,128)}, f32[3,64,1024]{2,1,0:T(8,128)S(1)}, u32[]{:S(2)}, u32[]{:S(2)}) %collective-permute-start.8) | collective-permute-done | bytes 786464 | tf_op jit(solution)/shard_map/ppermute | solution.py:533
  202.8 3.2 %collective-permute-done.9.refs_9_ = f32[3,64,1024]{2,1,0:T(8,128)S(1)} collective-permute-done((f32[3,64,1024]{2,1,0:T(8,128)}, f32[3,64,1024]{2,1,0:T(8,128)S(1)}, u32[]{:S(2)}, u32[]{:S(2)}) %collective-permute-start.9) | collective-permute-done | bytes 786464 | tf_op jit(solution)/shard_map/ppermute | solution.py:533
  206.0 0.9 copy-done.13
  206.9 6.2 %shard_map.60 = (f32[3,64,1024]{2,1,0:T(8,128)}, f32[3,64,1024]{2,1,0:T(8,128)}, f32[3,64,1024]{2,1,0:T(8,128)}, f32[3,64,1024]{2,1,0:T(8,128)}, f32[4,8,1024]{2,1,0:T(8,128)}) custom-call(f32[1,128,1024]{2,1,0:T(8,128)} %get-tuple-element.30.refs_0_, f32[1,128,1024]{2,1,0:T(8,128)} %copy-done, f32[1,128,1024]{2,1,0:T(8,128)} %copy-done.1, ...), custom_call_target="tpu_custom_call" | custom-call | flops 131072000 | bytes 9961472 | tf_op jit(solution)/shard_map/pallas_call | solution.py:474
  213.1 1.4 fusion
  214.5 0.1 reshape.11
  214.5 0.1 fusion.2
  214.7 1.2 collective-permute-done.21
  215.9 0.5 collective-permute-start.22
  216.4 0.5 collective-permute-start.19
  216.9 2.6 collective-permute-done.22
  219.4 1.0 collective-permute-start.23
  220.5 0.5 collective-permute-start.20
  220.9 3.0 %collective-permute-done.23 = f32[4,10]{1,0:T(4,128)S(1)} collective-permute-done((f32[4,10]{1,0:T(4,128)S(1)}, f32[4,10]{1,0:T(4,128)S(1)}, u32[]{:S(2)}, u32[]{:S(2)}) %collective-permute-start.23) | collective-permute-done | bytes 192 | tf_op jit(solution)/shard_map/ppermute | solution.py:538
  223.9 0.5 collective-permute-start.24
  224.5 0.5 collective-permute-start.25
  225.0 14.5 %collective-permute-done.24 = f32[4,10]{1,0:T(4,128)S(1)} collective-permute-done((f32[4,10]{1,0:T(4,128)S(1)}, f32[4,10]{1,0:T(4,128)S(1)}, u32[]{:S(2)}, u32[]{:S(2)}) %collective-permute-start.24) | collective-permute-done | bytes 192 | tf_op jit(solution)/shard_map/ppermute | solution.py:526
  239.4 1.2 collective-permute-start.26
  240.7 12.2 %collective-permute-done.25 = f32[4,10]{1,0:T(4,128)S(1)} collective-permute-done((f32[4,10]{1,0:T(4,128)S(1)}, f32[4,10]{1,0:T(4,128)S(1)}, u32[]{:S(2)}, u32[]{:S(2)}) %collective-permute-start.25) | collective-permute-done | bytes 192 | tf_op jit(solution)/shard_map/ppermute | solution.py:526
  252.8 0.5 collective-permute-start.10
  253.4 0.5 collective-permute-start.11
  253.9 2.4 collective-permute-start.12
  256.3 0.6 add_multiply_fusion
  257.0 0.8 copy-done.8
  257.8 0.3 copy-done.9
  258.1 4.7 %shard_map.63.refs_4_ = f32[4,512,1024]{2,1,0:T(8,128)} custom-call(f32[3,64,1024]{2,1,0:T(8,128)} %get-tuple-element.51.refs_0_, f32[3,64,1024]{2,1,0:T(8,128)} %copy-done.7, f32[3,64,1024]{2,1,0:T(8,128)} %copy-done.8, f32[3,64,1024]{2,1,0:T(8,128)} %copy-done.9, f32[4,512,1024]{2,1,0:T(8,128)} %get-tuple-element.55.refs_4_), custom_call_target="tpu_custom_call", output_to_operand_aliasing={{}: (4, {})} | custom-call | flops 6553600 | bytes 6291456 | tf_op jit(solution)/shard_map/pallas_call | solution.py:509
  262.8 10.6 %collective-permute-done.10.refs_1_ = f32[3,64,1024]{2,1,0:T(8,128)S(1)} collective-permute-done((f32[3,64,1024]{2,1,0:T(8,128)}, f32[3,64,1024]{2,1,0:T(8,128)S(1)}, u32[]{:S(2)}, u32[]{:S(2)}) %collective-permute-start.10) | collective-permute-done | bytes 786464 | tf_op jit(solution)/shard_map/ppermute | solution.py:526
  273.5 15.3 %collective-permute-done.11.refs_2_ = f32[3,64,1024]{2,1,0:T(8,128)} collective-permute-done((f32[3,64,1024]{2,1,0:T(8,128)}, f32[3,64,1024]{2,1,0:T(8,128)}, u32[]{:S(2)}, u32[]{:S(2)}) %collective-permute-start.11) | collective-permute-done | bytes 786464 | tf_op jit(solution)/shard_map/ppermute | solution.py:526
  288.7 4.7 %shard_map.64 = f32[4,512,1024]{2,1,0:T(8,128)} custom-call(f32[3,64,1024]{2,1,0:T(8,128)} %get-tuple-element.41.refs_0_, f32[3,64,1024]{2,1,0:T(8,128)} %copy-done.10, f32[3,64,1024]{2,1,0:T(8,128)} %collective-permute-done.11.refs_2_, f32[3,64,1024]{2,1,0:T(8,128)} %collective-permute-done.12.refs_3_, ...), custom_call_target="tpu_custom_call", output_to_operand_aliasing={{}: (4, {})} | custom-call | flops 6553600 | bytes 6291456 | tf_op jit(solution)/shard_map/pallas_call | solution.py:509
  (42 shorter events, 0.1 us)
Async XLA Ops:
  1.9 3.3 %collective-permute-start = (f32[4,32,1024]{2,1,0:T(8,128)S(1)}, f32[4,32,1024]{2,1,0:T(8,128)S(1)}, u32[]{:S(2)}, u32[]{:S(2)}) collective-permute-start(f32[4,32,1024]{2,1,0:T(8,128)S(1)} %get-tuple-element.59), channel_id=1, source_target_pairs={{0,1},{2,3},{4,5},{6,7},{8,9},{10,11},{12,13},{14,15},{16,17},{18,... | collective-permute-start | bytes 1572872 | tf_op jit(solution)/shard_map/ppermute | solution.py:533
  3.7 3.8 %collective-permute-start.1 = (f32[4,32,1024]{2,1,0:T(8,128)S(1)}, f32[4,32,1024]{2,1,0:T(8,128)S(1)}, u32[]{:S(2)}, u32[]{:S(2)}) collective-permute-start(f32[4,32,1024]{2,1,0:T(8,128)S(1)} %get-tuple-element.58), channel_id=1, source_target_pairs={{1,0},{3,2},{5,4},{7,6},{9,8},{11,10},{13,12},{15,14},{17,16},{19,... | collective-permute-start | bytes 1572872 | tf_op jit(solution)/shard_map/ppermute | solution.py:533
  5.2 2.3 copy-start.5
  7.5 0.8 copy-start.6
  28.3 56.7 %copy-start.17 = (f32[1,128,1024]{2,1,0:T(8,128)S(1)}, f32[1,128,1024]{2,1,0:T(8,128)}, u32[]{:S(2)}) copy-start(f32[1,128,1024]{2,1,0:T(8,128)} %get-tuple-element.32) | copy-start | bytes 1572868
  28.3 59.2 %collective-permute-start.2 = (f32[1,128,1024]{2,1,0:T(8,128)}, f32[1,128,1024]{2,1,0:T(8,128)S(1)}, u32[]{:S(2)}, u32[]{:S(2)}) collective-permute-start(f32[1,128,1024]{2,1,0:T(8,128)} %get-tuple-element.31), channel_id=1, source_target_pairs={{0,2},{2,0},{4,6},{6,4},{8,10},{10,8},{12,14},{14,12},{16,18},{18,... | collective-permute-start | bytes 1572872 | tf_op jit(solution)/shard_map/ppermute | solution.py:526
  83.5 33.5 %collective-permute-start.13 = (f32[3,64,1024]{2,1,0:T(8,128)}, f32[3,64,1024]{2,1,0:T(8,128)S(1)}, u32[]{:S(2)}, u32[]{:S(2)}) collective-permute-start(f32[3,64,1024]{2,1,0:T(8,128)} %get-tuple-element.46), channel_id=1, source_target_pairs={{0,2},{2,0},{4,6},{6,4},{8,10},{10,8},{12,14},{14,12},{16,18},{18,... | collective-permute-start | bytes 2359304 | tf_op jit(solution)/shard_map/ppermute | solution.py:526
  85.0 14.8 %collective-permute-start.3 = (f32[1,128,1024]{2,1,0:T(8,128)S(1)}, f32[1,128,1024]{2,1,0:T(8,128)S(1)}, u32[]{:S(2)}, u32[]{:S(2)}) collective-permute-start(f32[1,128,1024]{2,1,0:T(8,128)S(1)} %copy-done.17), channel_id=1, source_target_pairs={{0,4},{2,6},{4,0},{6,2},{8,12},{10,14},{12,8},{14,10},{16,20},{18,... | collective-permute-start | bytes 1572872 | tf_op jit(solution)/shard_map/ppermute | solution.py:526
  85.5 29.9 %collective-permute-start.4 = (f32[1,128,1024]{2,1,0:T(8,128)}, f32[1,128,1024]{2,1,0:T(8,128)S(1)}, u32[]{:S(2)}, u32[]{:S(2)}) collective-permute-start(f32[1,128,1024]{2,1,0:T(8,128)} %get-tuple-element.33), channel_id=1, source_target_pairs={{0,6},{2,4},{4,2},{6,0},{8,14},{10,12},{12,10},{14,8},{16,22},{18,... | collective-permute-start | bytes 1572872 | tf_op jit(solution)/shard_map/ppermute | solution.py:526
  87.0 57.8 %collective-permute-start.14 = (f32[3,64,1024]{2,1,0:T(8,128)}, f32[3,64,1024]{2,1,0:T(8,128)}, u32[]{:S(2)}, u32[]{:S(2)}) collective-permute-start(f32[3,64,1024]{2,1,0:T(8,128)} %get-tuple-element.47), channel_id=1, source_target_pairs={{0,4},{2,6},{4,0},{6,2},{8,12},{10,14},{12,8},{14,10},{16,20},{18,... | collective-permute-start | bytes 2359304 | tf_op jit(solution)/shard_map/ppermute | solution.py:526
  87.5 57.3 %copy-start = (f32[1,128,1024]{2,1,0:T(8,128)}, f32[1,128,1024]{2,1,0:T(8,128)S(1)}, u32[]{:S(2)}) copy-start(f32[1,128,1024]{2,1,0:T(8,128)S(1)} %collective-permute-done.2.refs_1_) | copy-start | bytes 1572868
  87.5 57.3 %collective-permute-start.15 = (f32[3,64,1024]{2,1,0:T(8,128)}, f32[3,64,1024]{2,1,0:T(8,128)}, u32[]{:S(2)}, u32[]{:S(2)}) collective-permute-start(f32[3,64,1024]{2,1,0:T(8,128)} %get-tuple-element.48), channel_id=1, source_target_pairs={{0,6},{2,4},{4,2},{6,0},{8,14},{10,12},{12,10},{14,8},{16,22},{18,... | collective-permute-start | bytes 2359304 | tf_op jit(solution)/shard_map/ppermute | solution.py:526
  99.8 45.1 %copy-start.1 = (f32[1,128,1024]{2,1,0:T(8,128)}, f32[1,128,1024]{2,1,0:T(8,128)S(1)}, u32[]{:S(2)}) copy-start(f32[1,128,1024]{2,1,0:T(8,128)S(1)} %collective-permute-done.3.refs_2_) | copy-start | bytes 1572868
  99.8 55.8 %collective-permute-start.5 = (f32[3,64,1024]{2,1,0:T(8,128)}, f32[3,64,1024]{2,1,0:T(8,128)S(1)}, u32[]{:S(2)}, u32[]{:S(2)}) collective-permute-start(f32[3,64,1024]{2,1,0:T(8,128)} %get-tuple-element.36), channel_id=1, source_target_pairs={{0,2},{2,0},{4,6},{6,4},{8,10},{10,8},{12,14},{14,12},{16,18},{18,... | collective-permute-start | bytes 2359304 | tf_op jit(solution)/shard_map/ppermute | solution.py:526
  115.4 29.4 %copy-start.2 = (f32[1,128,1024]{2,1,0:T(8,128)}, f32[1,128,1024]{2,1,0:T(8,128)S(1)}, u32[]{:S(2)}) copy-start(f32[1,128,1024]{2,1,0:T(8,128)S(1)} %collective-permute-done.4.refs_3_) | copy-start | bytes 1572868
  115.4 61.9 %collective-permute-start.6 = (f32[3,64,1024]{2,1,0:T(8,128)}, f32[3,64,1024]{2,1,0:T(8,128)}, u32[]{:S(2)}, u32[]{:S(2)}) collective-permute-start(f32[3,64,1024]{2,1,0:T(8,128)} %get-tuple-element.37), channel_id=1, source_target_pairs={{0,4},{2,6},{4,0},{6,2},{8,12},{10,14},{12,8},{14,10},{16,20},{18,... | collective-permute-start | bytes 2359304 | tf_op jit(solution)/shard_map/ppermute | solution.py:526
  117.0 27.9 %copy-start.3 = (f32[3,64,1024]{2,1,0:T(8,128)}, f32[3,64,1024]{2,1,0:T(8,128)S(1)}, u32[]{:S(2)}) copy-start(f32[3,64,1024]{2,1,0:T(8,128)S(1)} %collective-permute-done.13.refs_5_) | copy-start | bytes 2359300
  117.0 60.4 %collective-permute-start.7 = (f32[3,64,1024]{2,1,0:T(8,128)}, f32[3,64,1024]{2,1,0:T(8,128)}, u32[]{:S(2)}, u32[]{:S(2)}) collective-permute-start(f32[3,64,1024]{2,1,0:T(8,128)} %get-tuple-element.38), channel_id=1, source_target_pairs={{0,6},{2,4},{4,2},{6,0},{8,14},{10,12},{12,10},{14,8},{16,22},{18,... | collective-permute-start | bytes 2359304 | tf_op jit(solution)/shard_map/ppermute | solution.py:526
  149.7 38.5 %collective-permute-start.16 = (f32[3,64,1024]{2,1,0:T(8,128)}, f32[3,64,1024]{2,1,0:T(8,128)S(1)}, u32[]{:S(2)}, u32[]{:S(2)}) collective-permute-start(f32[3,64,1024]{2,1,0:T(8,128)} %get-tuple-element.49), channel_id=1, source_target_pairs={{0,8},{2,10},{4,12},{6,14},{8,16},{10,18},{12,20},{14,22},{16,24},... | collective-permute-start | bytes 2359304 | tf_op jit(solution)/shard_map/ppermute | solution.py:533
  153.2 35.1 %collective-permute-start.17 = (f32[3,64,1024]{2,1,0:T(8,128)}, f32[3,64,1024]{2,1,0:T(8,128)}, u32[]{:S(2)}, u32[]{:S(2)}) collective-permute-start(f32[3,64,1024]{2,1,0:T(8,128)} %get-tuple-element.50), channel_id=1, source_target_pairs={{8,0},{10,2},{12,4},{14,6},{16,8},{18,10},{20,12},{22,14},{24,16},... | collective-permute-start | bytes 2359304 | tf_op jit(solution)/shard_map/ppermute | solution.py:533
  155.6 21.7 %copy-start.4 = (f32[3,64,1024]{2,1,0:T(8,128)}, f32[3,64,1024]{2,1,0:T(8,128)S(1)}, u32[]{:S(2)}) copy-start(f32[3,64,1024]{2,1,0:T(8,128)S(1)} %collective-permute-done.5.refs_5_) | copy-start | bytes 2359300
  182.2 30.9 %copy-start.14 = (f32[1024,8]{1,0:T(8,128)S(1)}, f32[1024,8]{1,0:T(8,128)}, u32[]{:S(2)}) copy-start(f32[1024,8]{1,0:T(8,128)} %constant.6.clone) | copy-start | bytes 98308
  182.2 32.3 %copy-start.15 = (f32[64,10]{1,0:T(8,128)S(1)}, f32[64,10]{1,0:T(8,128)}, u32[]{:S(2)}) copy-start(f32[64,10]{1,0:T(8,128)} %constant.7.clone) | copy-start | bytes 7684
  182.2 74.1 %copy-start.16 = (f32[4,10]{1,0:T(4,128)S(1)}, f32[4,10]{1,0:T(4,128)}, u32[]{:S(2)}) copy-start(f32[4,10]{1,0:T(4,128)} %constant.10) | copy-start | bytes 484
  182.2 20.6 %collective-permute-start.8 = (f32[3,64,1024]{2,1,0:T(8,128)}, f32[3,64,1024]{2,1,0:T(8,128)S(1)}, u32[]{:S(2)}, u32[]{:S(2)}) collective-permute-start(f32[3,64,1024]{2,1,0:T(8,128)} %get-tuple-element.39), channel_id=1, source_target_pairs={{0,8},{2,10},{4,12},{6,14},{8,16},{10,18},{12,20},{14,22},{16,24},... | collective-permute-start | bytes 2359304 | tf_op jit(solution)/shard_map/ppermute | solution.py:533
  185.9 20.2 %collective-permute-start.9 = (f32[3,64,1024]{2,1,0:T(8,128)}, f32[3,64,1024]{2,1,0:T(8,128)S(1)}, u32[]{:S(2)}, u32[]{:S(2)}) collective-permute-start(f32[3,64,1024]{2,1,0:T(8,128)} %get-tuple-element.40), channel_id=1, source_target_pairs={{8,0},{10,2},{12,4},{14,6},{16,8},{18,10},{20,12},{22,14},{24,16},... | collective-permute-start | bytes 2359304 | tf_op jit(solution)/shard_map/ppermute | solution.py:533
  188.3 0.9 copy-start.12
  195.4 58.5 %collective-permute-start.18 = (f32[3,64,1024]{2,1,0:T(8,128)}, f32[3,64,1024]{2,1,0:T(8,128)S(1)}, u32[]{:S(2)}, u32[]{:S(2)}) collective-permute-start(f32[3,64,1024]{2,1,0:T(8,128)} %get-tuple-element.52), channel_id=1, source_target_pairs={{0,2},{2,0},{4,6},{6,4},{8,10},{10,8},{12,14},{14,12},{16,18},{18,... | collective-permute-start | bytes 2359304 | tf_op jit(solution)/shard_map/ppermute | solution.py:526
  202.8 3.2 %copy-start.11 = (f32[3,64,1024]{2,1,0:T(8,128)}, f32[3,64,1024]{2,1,0:T(8,128)S(1)}, u32[]{:S(2)}) copy-start(f32[3,64,1024]{2,1,0:T(8,128)S(1)} %collective-permute-done.8.refs_8_) | copy-start | bytes 2359300
  206.0 0.9 copy-start.13
  214.7 1.2 collective-permute-start.21
  215.9 3.6 %collective-permute-start.22 = (f32[4,10]{1,0:T(4,128)S(1)}, f32[4,10]{1,0:T(4,128)S(1)}, u32[]{:S(2)}, u32[]{:S(2)}) collective-permute-start(f32[4,10]{1,0:T(4,128)S(1)} %add.22), channel_id=1, source_target_pairs={{0,8},{2,10},{4,12},{6,14},{8,0},{10,2},{12,4},{14,6},{16,24},{18,... | collective-permute-start | bytes 488 | tf_op jit(solution)/shard_map/ppermute | solution.py:538
  216.4 40.6 %collective-permute-start.19 = (f32[3,64,1024]{2,1,0:T(8,128)}, f32[3,64,1024]{2,1,0:T(8,128)S(1)}, u32[]{:S(2)}, u32[]{:S(2)}) collective-permute-start(f32[3,64,1024]{2,1,0:T(8,128)} %get-tuple-element.53), channel_id=1, source_target_pairs={{0,4},{2,6},{4,0},{6,2},{8,12},{10,14},{12,8},{14,10},{16,20},{18,... | collective-permute-start | bytes 2359304 | tf_op jit(solution)/shard_map/ppermute | solution.py:526
  219.4 4.5 %collective-permute-start.23 = (f32[4,10]{1,0:T(4,128)S(1)}, f32[4,10]{1,0:T(4,128)S(1)}, u32[]{:S(2)}, u32[]{:S(2)}) collective-permute-start(f32[4,10]{1,0:T(4,128)S(1)} %add.23), channel_id=1, source_target_pairs={{0,16},{2,18},{4,20},{6,22},{8,24},{10,26},{12,28},{14,30},{16,0},... | collective-permute-start | bytes 488 | tf_op jit(solution)/shard_map/ppermute | solution.py:538
  220.5 36.5 %collective-permute-start.20 = (f32[3,64,1024]{2,1,0:T(8,128)}, f32[3,64,1024]{2,1,0:T(8,128)S(1)}, u32[]{:S(2)}, u32[]{:S(2)}) collective-permute-start(f32[3,64,1024]{2,1,0:T(8,128)} %get-tuple-element.54), channel_id=1, source_target_pairs={{0,6},{2,4},{4,2},{6,0},{8,14},{10,12},{12,10},{14,8},{16,22},{18,... | collective-permute-start | bytes 2359304 | tf_op jit(solution)/shard_map/ppermute | solution.py:526
  223.9 15.5 %collective-permute-start.24 = (f32[4,10]{1,0:T(4,128)S(1)}, f32[4,10]{1,0:T(4,128)S(1)}, u32[]{:S(2)}, u32[]{:S(2)}) collective-permute-start(f32[4,10]{1,0:T(4,128)S(1)} %add.24), channel_id=1, source_target_pairs={{0,2},{2,0},{4,6},{6,4},{8,10},{10,8},{12,14},{14,12},{16,18},{18,... | collective-permute-start | bytes 488 | tf_op jit(solution)/shard_map/ppermute | solution.py:526
  224.5 28.4 %collective-permute-start.25 = (f32[4,10]{1,0:T(4,128)S(1)}, f32[4,10]{1,0:T(4,128)S(1)}, u32[]{:S(2)}, u32[]{:S(2)}) collective-permute-start(f32[4,10]{1,0:T(4,128)S(1)} %add.24), channel_id=1, source_target_pairs={{0,4},{2,6},{4,0},{6,2},{8,12},{10,14},{12,8},{14,10},{16,20},{18,... | collective-permute-start | bytes 488 | tf_op jit(solution)/shard_map/ppermute | solution.py:526
  239.4 13.9 %collective-permute-start.26 = (f32[4,10]{1,0:T(4,128)S(1)}, f32[4,10]{1,0:T(4,128)S(1)}, u32[]{:S(2)}, u32[]{:S(2)}) collective-permute-start(f32[4,10]{1,0:T(4,128)S(1)} %add.24), channel_id=1, source_target_pairs={{0,6},{2,4},{4,2},{6,0},{8,14},{10,12},{12,10},{14,8},{16,22},{18,... | collective-permute-start | bytes 488 | tf_op jit(solution)/shard_map/ppermute | solution.py:526
  252.8 20.6 %collective-permute-start.10 = (f32[3,64,1024]{2,1,0:T(8,128)}, f32[3,64,1024]{2,1,0:T(8,128)S(1)}, u32[]{:S(2)}, u32[]{:S(2)}) collective-permute-start(f32[3,64,1024]{2,1,0:T(8,128)} %get-tuple-element.42), channel_id=1, source_target_pairs={{0,2},{2,0},{4,6},{6,4},{8,10},{10,8},{12,14},{14,12},{16,18},{18,... | collective-permute-start | bytes 2359304 | tf_op jit(solution)/shard_map/ppermute | solution.py:526
  253.4 35.4 %collective-permute-start.11 = (f32[3,64,1024]{2,1,0:T(8,128)}, f32[3,64,1024]{2,1,0:T(8,128)}, u32[]{:S(2)}, u32[]{:S(2)}) collective-permute-start(f32[3,64,1024]{2,1,0:T(8,128)} %get-tuple-element.43), channel_id=1, source_target_pairs={{0,4},{2,6},{4,0},{6,2},{8,12},{10,14},{12,8},{14,10},{16,20},{18,... | collective-permute-start | bytes 2359304 | tf_op jit(solution)/shard_map/ppermute | solution.py:526
  253.9 3.1 %copy-start.7 = (f32[3,64,1024]{2,1,0:T(8,128)}, f32[3,64,1024]{2,1,0:T(8,128)S(1)}, u32[]{:S(2)}) copy-start(f32[3,64,1024]{2,1,0:T(8,128)S(1)} %collective-permute-done.18.refs_1_) | copy-start | bytes 2359300
  253.9 34.9 %collective-permute-start.12 = (f32[3,64,1024]{2,1,0:T(8,128)}, f32[3,64,1024]{2,1,0:T(8,128)}, u32[]{:S(2)}, u32[]{:S(2)}) collective-permute-start(f32[3,64,1024]{2,1,0:T(8,128)} %get-tuple-element.44), channel_id=1, source_target_pairs={{0,6},{2,4},{4,2},{6,0},{8,14},{10,12},{12,10},{14,8},{16,22},{18,... | collective-permute-start | bytes 2359304 | tf_op jit(solution)/shard_map/ppermute | solution.py:526
  256.9 0.9 copy-start.8
  256.9 1.2 copy-start.9
  273.5 15.3 %copy-start.10 = (f32[3,64,1024]{2,1,0:T(8,128)}, f32[3,64,1024]{2,1,0:T(8,128)S(1)}, u32[]{:S(2)}) copy-start(f32[3,64,1024]{2,1,0:T(8,128)S(1)} %collective-permute-done.10.refs_1_) | copy-start | bytes 2359300

commit v2 on v1

v2 whole, which is shorter than its diff:
```python
import functools

import jax
import jax.numpy as jnp
import numpy as np
from jax import lax
from jax.experimental import pallas as pl
from jax.experimental.pallas import tpu as pltpu
from jax.sharding import PartitionSpec as P


SLEVELS = 3
TLEVELS = 3

LIFT_ALPHA = -1.586134342
LIFT_BETA = -0.05298011854
LIFT_GAMMA = 0.8829110762
LIFT_DELTA = 0.4435068522
LIFT_ZETA = 1.149604398
FACTORS = (LIFT_ALPHA, LIFT_BETA, LIFT_GAMMA, LIFT_DELTA)

LANES = 128
SUB = 8
WIDE = 2 * LANES
TILE_ROWS = 384
HALO = 32
PAD = SUB
SPAN = 2 * 2**TLEVELS
KEPT = (0, 2, 3)


def level_of(number, ceiling):
    depth_now = 1
    while number % 2 == 0 and depth_now <= ceiling:
        number = number // 2
        depth_now = depth_now + 1
    return depth_now


def space_table(levels):
    period = 2**levels
    band_table = np.zeros((period * period, 3 * levels + 1), np.float32)
    for row_pos in range(period):
        for col_pos in range(period):
            row_level = level_of(row_pos, levels)
            col_level = level_of(col_pos, levels)
            finest = min(row_level, col_level)
            if finest > levels:
                column = 3 * levels
            elif row_level == col_level:
                column = 3 * (finest - 1) + 2
            elif row_level == finest:
                column = 3 * (finest - 1)
            else:
                column = 3 * (finest - 1) + 1
            band_table[row_pos * period + col_pos, column] = 1.0
    return band_table


def time_table(levels):
    period = 2**levels
    band_table = np.zeros((period, levels + 1), np.float32)
    for number in range(period):
        band_table[number, level_of(number, levels) - 1] = 1.0
    return band_table


def band_means(totals, frames_all, rows_all, cols_all, levels_s, levels_t):
    space_share = space_table(levels_s).sum(0) / float((2**levels_s) ** 2)
    time_share = time_table(levels_t).sum(0) / float(2**levels_t)
    counts = (
        float(frames_all) * float(rows_all) * float(cols_all) * np.outer(time_share, space_share)
    )
    return totals / jnp.asarray(counts, jnp.float32)


def lift_rows(buf, count):
    groups = count // SUB

    def step(odd, factor):
        target, near, far = (1, 0, 2) if odd else (0, -1, 1)

        def body(k, carry):
            top = PAD + 2 * SUB * k
            at = pl.ds(top + target, SUB, stride=2)
            for j in range(buf.shape[0]):
                buf[j, at, :] = buf[j, at, :] + factor * (
                    buf[j, pl.ds(top + near, SUB, stride=2), :]
                    + buf[j, pl.ds(top + far, SUB, stride=2), :]
                )
            return carry

        lax.fori_loop(0, groups, body, 0, unroll=5)

    step(True, LIFT_ALPHA)
    step(False, LIFT_BETA)
    step(True, LIFT_GAMMA)
    step(False, LIFT_DELTA)


def filter_taps():
    size = 8 * len(FACTORS)
    lifted = np.eye(size)
    for count, factor in enumerate(FACTORS):
        for n in range(1 - count % 2, size - 1, 2):
            lifted[n] += factor * (lifted[n - 1] + lifted[n + 1])
    middle = size // 2
    reach = len(FACTORS) + 1
    low = [lifted[middle, middle + k] * LIFT_ZETA for k in range(reach)]
    high = [lifted[middle + 1, middle + 1 + k] / LIFT_ZETA for k in range(reach)]
    return low, high


def column_weights(stride):
    low, high = filter_taps()
    band = np.zeros((WIDE + 2 * LANES, WIDE))
    for n in range(0, WIDE, stride):
        taps = low if n // stride % 2 == 0 else high
        for k, tap in enumerate(taps):
            band[LANES + n + k * stride, n] = tap
            band[LANES + n - k * stride, n] = tap
    upper = band.astype(jnp.bfloat16)
    lower = (band - upper.astype(np.float64)).astype(jnp.bfloat16)
    return np.concatenate([upper, lower])


def filter_cols(buf, rows, level, weights, split):
    blocks = buf.shape[0]
    stride = 2**level
    upper, lower = split
    lane = lax.broadcasted_iota(jnp.int32, (2 * SUB, LANES), 1)
    sub = lax.broadcasted_iota(jnp.int32, (2 * SUB, LANES), 0)
    scale = jnp.where(sub % 2 == 0, jnp.float32(LIFT_ZETA), jnp.float32(1.0 / LIFT_ZETA))
    before = (LANES - lane) % LANES
    after = (2 * LANES - 2 * stride - lane) % LANES

    def halves(i, carry):
        at = pl.ds(pl.multiple_of(2 * SUB * i, 2 * SUB), 2 * SUB)
        v = [buf[j, pl.ds(PAD + 2 * SUB * i, 2 * SUB), :] * scale for j in range(blocks)]
        left = jnp.take_along_axis(v[0], before, axis=1)
        right = jnp.take_along_axis(v[-1], after, axis=1)
        for j, x in enumerate([left] + v + [right]):
            c = slice(j * LANES, (j + 1) * LANES)
            top = x.astype(jnp.bfloat16)
            upper[at, c] = top
            lower[at, c] = (x - top.astype(jnp.float32)).astype(jnp.bfloat16)
        return carry

    lax.fori_loop(0, rows // (2 * SUB), halves, 0, unroll=5)
    depth = WIDE + 2 * LANES
    heavy, light = weights[level, :depth], weights[level, depth:]
    factor = jnp.concatenate([heavy, heavy, light])
    tile = min(rows, TILE_ROWS)
    across = blocks * LANES // WIDE

    def block(i, carry):
        r = pl.multiple_of(i // across * tile, SUB)
        n = i % across
        k = pl.ds(pl.multiple_of(n * WIDE, WIDE), depth)
        at = pl.ds(pl.multiple_of(r, 2 * SUB), tile)
        x, rest = upper[at, k], lower[at, k]
        y = jnp.dot(
            jnp.concatenate([x, rest, x], axis=1), factor, preferred_element_type=jnp.float32
        )
        for h in range(WIDE // LANES):
            buf[n * (WIDE // LANES) + h, pl.ds(PAD + r, tile), :] = y[:, h * LANES : (h + 1) * LANES]
        return carry

    lax.fori_loop(0, rows // tile * across, block, 0, unroll=4)


def spatial_frame(load, strip, rows, weights, scratch):
    bufs, split = scratch[:SLEVELS], scratch[SLEVELS:]
    row_index = lax.axis_index("row")
    is_first = row_index == 0
    is_last = row_index == lax.axis_size("row") - 1
    b = bufs[0]
    places = segment_places(strip)
    for at, (start, count) in zip(places, strip):
        first = PAD + at
        load(b, first - HALO, start - HALO, count + 2 * HALO)
        if start == 0:

            @pl.when(is_first)
            def _(first=first):
                for j in range(1, HALO):
                    b[:, first - j : first - j + 1, :] = b[:, first + j : first + j + 1, :]

    total = buffer_rows(strip)
    for level in range(SLEVELS):
        b = bufs[level]
        stride = 2**level
        for at, (start, count) in zip(places, strip):
            if start + count == rows:

                @pl.when(is_last)
                def _(b=b, stop=PAD + (at + count) // stride, level=level):
                    inner = HALO // 2**level
                    for j in range(inner - 1 if level == 0 else inner * 5 // 8):
                        b[:, stop + j : stop + j + 1, :] = b[:, stop - 2 - j : stop - 1 - j, :]

        lift_rows(b, total // stride // 2)
        filter_cols(b, total // stride, level, weights, split)
        if level + 1 < SLEVELS:
            low = bufs[level + 1]

            def body(k, carry, b=b, low=low):
                for j in range(b.shape[0]):
                    low[j, pl.ds(PAD + SUB * k, SUB), :] = b[
                        j, pl.ds(PAD + 2 * SUB * k, SUB, stride=2), :
                    ]
                return carry

            lax.fori_loop(0, total // stride // 2 // SUB, body, 0, unroll=5)
    lane = lax.broadcasted_iota(jnp.int32, (SUB, LANES), 1)
    for level in reversed(range(SLEVELS - 1)):
        b, low = bufs[level], bufs[level + 1]
        stride = 2 ** (level + 1)
        keep = lane % stride == 0
        for at, (_, count) in zip(places, strip):

            def body(k, carry, b=b, low=low, keep=keep, stride=stride, at=at):
                outer = pl.ds(PAD + at // (stride // 2) + 2 * SUB * k, SUB, stride=2)
                inner = pl.ds(PAD + at // stride + SUB * k, SUB)
                for j in range(b.shape[0]):
                    b[j, outer, :] = jnp.where(keep, low[j, inner, :], b[j, outer, :])
                return carry

            lax.fori_loop(0, count // stride // SUB, body, 0, unroll=4)


def strips_of(rows):
    edge = rows // 4
    return [[(edge, rows - 2 * edge)], [(0, edge), (rows - edge, edge)]]


def strip_rows(strip):
    return sum(count for _, count in strip)


def buffer_rows(strip):
    return sum(count + 2 * HALO for _, count in strip)


def segment_places(strip):
    places, at = [], 0
    for _, count in strip:
        places.append(at + HALO)
        at += count + 2 * HALO
    return places


def part_start(starts, strip, owner, group):
    part = strip_rows(strip) // group
    where = owner * part + starts[0]
    passed = 0
    for k in range(1, len(strip)):
        passed += strip[k - 1][1]
        where = jnp.where(owner * part >= passed, owner * part - passed + starts[k], where)
    return where


def member(group):
    return lax.axis_index("frame") % group


UNITS = ((0, (0,)), (0, (1,)), (0, (2, 3)), (1, (0, 1)), (1, (2, 3)))


def turns_of(strips, group):
    middle = strip_rows(strips[0]) // group
    outer = strip_rows(strips[1]) // group
    return [(0, 0, middle), (1, 0, outer // 2), (1, outer // 2, outer // 2)]


def space_kernel(group, strip, rows, *refs):
    inner = all(start > 0 and start + count < rows for start, count in strip)
    x_ref = refs[0].at[0]
    top_ref, bottom_ref = (None, None) if inner else (refs[1].at[0], refs[2].at[0])
    refs = refs[1:] if inner else refs[3:]
    weights, pieces, scratch = refs[0], refs[1 : 1 + group], refs[1 + group :]

    def load(b, to, start, count):
        spans = []
        if start < 0:
            spans.append((top_ref, 0, HALO, to))
            start, count, to = start + HALO, count - HALO, to + HALO
        if start + count > rows:
            spans.append((bottom_ref, 0, HALO, to + count - HALO))
            count -= HALO
        spans.append((x_ref, start, count, to))
        for j in range(b.shape[0]):
            c = slice(j * LANES, (j + 1) * LANES)
            for source, begin, length, place in spans:
                b[j, place : place + length, :] = source[begin : begin + length, c]

    spatial_frame(load, strip, rows, weights, scratch)
    me = member(group)
    part = strip_rows(strip) // group
    starts = [PAD + at for at in segment_places(strip)]
    for d in range(group):
        start = pl.multiple_of(part_start(starts, strip, me ^ d, group), SUB)
        for j in range(scratch[0].shape[0]):
            c = slice(j * LANES, (j + 1) * LANES)
            pieces[d][0, :, c] = scratch[0][j, pl.ds(start, part), :]


def space(unit, footage, top, bottom, weights, strips, group):
    which, chosen = UNITS[unit]
    strip = strips[which]
    _, rows, width = footage.shape
    part = strip_rows(strip) // group
    total = buffer_rows(strip)
    f32 = jnp.float32
    shift = chosen[0]

    def frame(height):
        return pl.BlockSpec((1, height, width), lambda g: (g + shift, 0, 0))

    inner = all(start > 0 and start + count < rows for start, count in strip)
    given = [footage] if inner else [footage, top, bottom]
    specs = [frame(rows)] if inner else [frame(rows), frame(HALO), frame(HALO)]
    shapes = [
        pltpu.VMEM((width // LANES, total // 2**level + 2 * PAD, LANES), f32)
        for level in range(SLEVELS)
    ] + [pltpu.VMEM((total, width + 2 * LANES), jnp.bfloat16)] * 2
    return pl.pallas_call(
        functools.partial(space_kernel, group, strip, rows),
        grid=(len(chosen),),
        in_specs=specs + [pl.BlockSpec(weights.shape, lambda g: (0, 0, 0))],
        out_specs=[pl.BlockSpec((1, part, width), lambda g: (g, 0, 0))] * group,
        out_shape=[jax.ShapeDtypeStruct((len(chosen), part, width), f32)] * group,
        scratch_shapes=shapes,
        cost_estimate=pl.CostEstimate(
            flops=len(chosen) * rows * width * 400,
            bytes_accessed=len(chosen) * rows * width * 8,
            transcendentals=0,
        ),
    )(*given, weights)


BLOCK_ROWS = 32


def each_member(group, body):
    me = member(group)
    for place in range(group):
        pl.when(me == place)(functools.partial(body, place))


def span_of(group, chosen, refs, place):
    frames = SPAN // group
    found = []
    for n in range(SPAN):
        d, f = place ^ (n // frames), n % frames
        u = [f in own for own in chosen].index(True)
        found.append((refs[u * group + d], chosen[u].index(f)))
    return found


def each_tile(rows, width, body):
    tiles = width // WIDE

    def step(k, carry):
        r = pl.multiple_of((k // tiles) * SUB, SUB)
        c = pl.multiple_of((k % tiles) * WIDE, WIDE)
        body(pl.ds(r, SUB), pl.ds(c, WIDE))
        return carry

    lax.fori_loop(0, rows // SUB * tiles, step, 0)


def partial_levels(x):
    o = {n: x[n] - 0.5 * (x[n - 1] + x[n + 1]) for n in range(1, SPAN - 1, 2)}
    o[15] = x[15] - 0.5 * x[14]
    low = {n: x[n] + 0.25 * (o[n - 1] + o[n + 1]) for n in range(2, SPAN, 2)}
    low[0] = x[0] + 0.25 * o[1]
    p = {n: low[n] - 0.5 * (low[n - 2] + low[n + 2]) for n in (2, 6, 10)}
    p[14] = low[14] - 0.5 * low[12]
    m = {n: low[n] + 0.25 * (p[n - 2] + p[n + 2]) for n in (8, 12)}
    m[0] = low[0] + 0.25 * p[2]
    q12 = m[12] - 0.5 * m[8]
    to_right = (o[15], p[14], q12)
    to_left = (x[0], low[0], m[0])
    return to_right, to_left


def full_levels(x, left, right, is_first, is_last):
    a0, b0, c0 = left
    x16, low16, m16 = right
    o = {n: x[n] - 0.5 * (x[n - 1] + x[n + 1]) for n in range(1, SPAN - 1, 2)}
    o[15] = x[15] - 0.5 * (x[14] + jnp.where(is_last, x[14], x16))
    before = jnp.where(is_first, o[1], a0 - 0.5 * x[0])
    low = {n: x[n] + 0.25 * (o[n - 1] + o[n + 1]) for n in range(2, SPAN, 2)}
    low[0] = x[0] + 0.25 * (before + o[1])
    p = {n: low[n] - 0.5 * (low[n - 2] + low[n + 2]) for n in (2, 6, 10)}
    p[14] = low[14] - 0.5 * (low[12] + jnp.where(is_last, low[12], low16 + 0.25 * o[15]))
    before = jnp.where(is_first, p[2], b0 - 0.125 * x[0] - 0.5 * low[0])
    m = {n: low[n] + 0.25 * (p[n - 2] + p[n + 2]) for n in (4, 8, 12)}
    m[0] = low[0] + 0.25 * (before + p[2])
    q4 = m[4] - 0.5 * (m[0] + m[8])
    after = jnp.where(is_last, m[8], m16 + 0.21875 * o[15] + 0.25 * p[14])
    q12 = m[12] - 0.5 * (m[8] + after)
    before = jnp.where(is_first, q4, c0 - 0.03125 * x[0] - 0.125 * low[0] - 0.5 * m[0])
    y = dict(o)
    y.update(p)
    y[4] = q4
    y[12] = q12
    y[0] = m[0] + 0.25 * (before + q4)
    y[8] = m[8] + 0.25 * (q4 + q12)
    return [y[n] for n in range(SPAN)]


def edges_kernel(group, chosen, *refs):
    given = len(chosen) * group
    to_right, to_left = refs[given:]
    _, rows, width = to_right.shape

    def variant(place):
        span = span_of(group, chosen, refs[:given], place)

        def body(r, c):
            right, left = partial_levels([ref[k, r, c] for ref, k in span])
            for k in range(TLEVELS):
                to_right[k, r, c] = right[k]
                to_left[k, r, c] = left[k]

        each_tile(rows, width, body)

    each_member(group, variant)


def time_kernel(group, chosen, *refs):
    given = len(chosen) * group
    left, right = refs[given : given + 2]
    pieces = refs[given + 2 : given + 2 + group]
    power = refs[given + 2 + group]
    frames = SPAN // group
    _, rows, width = left.shape
    spot = lax.axis_index("frame") // group
    is_first = spot == 0
    is_last = spot == lax.axis_size("frame") // group - 1

    @pl.when(pl.program_id(0) == 0)
    def _():
        power[...] = jnp.zeros_like(power)

    def variant(place):
        span = span_of(group, chosen, refs[:given], place)

        def body(r, c):
            y = full_levels(
                [ref[k, r, c] for ref, k in span],
                [left[k, r, c] for k in range(TLEVELS)],
                [right[k, r, c] for k in range(TLEVELS)],
                is_first,
                is_last,
            )
            sums = [None] * (TLEVELS + 1)
            for n in range(SPAN):
                t = level_of(n % 2**TLEVELS, TLEVELS) - 1
                square = y[n] * y[n]
                sums[t] = square if sums[t] is None else sums[t] + square
                if n % frames in KEPT:
                    pieces[place ^ (n // frames)][KEPT.index(n % frames), r, c] = y[n]
            for t in range(TLEVELS + 1):
                power[t, :, c] = power[t, :, c] + sums[t]

        each_tile(rows, width, body)

    each_member(group, variant)


def span_specs(group, chosen, first, width):
    skip = first // BLOCK_ROWS
    return [
        pl.BlockSpec((len(frames), BLOCK_ROWS, width), lambda i: (0, skip + i, 0))
        for frames in chosen
        for _ in range(group)
    ]


def time_cost(rows, width, frames):
    return pl.CostEstimate(
        flops=rows * width * 2000, bytes_accessed=rows * width * 4 * frames, transcendentals=0
    )


def edges(group, first, rows, chosen, given):
    width = given[0].shape[2]
    spec = pl.BlockSpec((TLEVELS, BLOCK_ROWS, width), lambda i: (0, i, 0))
    shape = jax.ShapeDtypeStruct((TLEVELS, rows, width), jnp.float32)
    return pl.pallas_call(
        functools.partial(edges_kernel, group, chosen),
        grid=(rows // BLOCK_ROWS,),
        in_specs=span_specs(group, chosen, first, width),
        out_specs=[spec, spec],
        out_shape=[shape, shape],
        cost_estimate=time_cost(rows, width, SPAN + 6),
    )(*given)


def finish_time(group, first, rows, chosen, given, left, right):
    width = given[0].shape[2]
    kept = len(KEPT)
    halo = pl.BlockSpec((TLEVELS, BLOCK_ROWS, width), lambda i: (0, i, 0))
    outs = pl.pallas_call(
        functools.partial(time_kernel, group, chosen),
        grid=(rows // BLOCK_ROWS,),
        in_specs=span_specs(group, chosen, first, width) + [halo, halo],
        out_specs=[pl.BlockSpec((kept, BLOCK_ROWS, width), lambda i: (0, i, 0))] * group
        + [pl.BlockSpec((TLEVELS + 1, SUB, width), lambda i: (0, 0, 0))],
        out_shape=[jax.ShapeDtypeStruct((kept, rows, width), jnp.float32)] * group
        + [jax.ShapeDtypeStruct((TLEVELS + 1, SUB, width), jnp.float32)],
        cost_estimate=time_cost(rows, width, 2 * SPAN + 6),
    )(*given, left, right)
    return outs[:group], outs[group]


def home_kernel(group, strip, fresh, *refs):
    given = 3 * group
    out, held, sems = refs[given if fresh else given + 1 :]
    me = member(group)
    starts = [start for start, _ in strip]
    step = pl.program_id(0)

    def copy(d, at):
        start = part_start(starts, strip, me ^ d, group) + at * BLOCK_ROWS
        return pltpu.make_async_copy(
            held.at[at, d],
            out.at[1, pl.ds(pl.multiple_of(start, SUB), BLOCK_ROWS)],
            sems.at[at, d],
        )

    for d in range(group):
        held[step, d] = refs[group + d][0] - 0.5 * (refs[d][0] + refs[2 * group + d][0])
        copy(d, step).start()

    @pl.when(step == held.shape[0] - 1)
    def _():
        for at in range(held.shape[0]):
            for d in range(group):
                copy(d, at).wait()


def home(group, strip, chosen, sent, shape, coeffs):
    width = shape[2]
    part = strip_rows(strip) // group
    given, specs = [], []
    for f in range(3):
        u = [f in frames for frames in chosen].index(True)
        k = chosen[u].index(f)
        given += sent[u]
        specs += [pl.BlockSpec((1, BLOCK_ROWS, width), lambda i, k=k: (k, i, 0))] * group
    fresh = coeffs is None
    if not fresh:
        given.append(coeffs)
        specs.append(pl.BlockSpec(memory_space=pl.ANY))
    return pl.pallas_call(
        functools.partial(home_kernel, group, strip, fresh),
        grid=(part // BLOCK_ROWS,),
        in_specs=specs,
        out_specs=pl.BlockSpec(memory_space=pl.ANY),
        out_shape=jax.ShapeDtypeStruct(shape, jnp.float32),
        input_output_aliases={} if fresh else {3 * group: 0},
        scratch_shapes=[
            pltpu.VMEM((part // BLOCK_ROWS, group, BLOCK_ROWS, width), jnp.float32),
            pltpu.SemaphoreType.DMA((part // BLOCK_ROWS, group)),
        ],
        cost_estimate=time_cost(part, width, 4 * group),
    )(*given)


def place_kernel(group, strip, first, *refs):
    pieces, _, out, held, ins, outs = refs[:group], *refs[group:]
    kept, rows, _ = pieces[0].shape
    me = member(group)
    starts = [start for start, _ in strip]
    arriving, leaving = [], []
    for d in range(group):
        start = pl.multiple_of(part_start(starts, strip, me ^ d, group) + first, SUB)
        for k, f in enumerate(KEPT):
            n = d * kept + k
            arriving.append(pltpu.make_async_copy(pieces[d].at[k], held.at[n], ins.at[n]))
            leaving.append(
                pltpu.make_async_copy(held.at[n], out.at[f, pl.ds(start, rows)], outs.at[n])
            )
    for copy in arriving:
        copy.start()
    for copy, after in zip(arriving, leaving):
        copy.wait()
        after.start()
    for copy in leaving:
        copy.wait()


def place(group, strip, first, pieces, coeffs):
    kept, rows, width = pieces[0].shape
    count = group * kept
    return pl.pallas_call(
        functools.partial(place_kernel, group, strip, first),
        in_specs=[pl.BlockSpec(memory_space=pl.ANY)] * (group + 1),
        out_specs=pl.BlockSpec(memory_space=pl.ANY),
        out_shape=jax.ShapeDtypeStruct(coeffs.shape, coeffs.dtype),
        input_output_aliases={group: 0},
        scratch_shapes=[
            pltpu.VMEM((count, rows, width), jnp.float32),
            pltpu.SemaphoreType.DMA((count,)),
            pltpu.SemaphoreType.DMA((count,)),
        ],
        cost_estimate=time_cost(rows, width, 2 * count),
    )(*pieces, coeffs)


def swap(blocks, group):
    devices = range(lax.axis_size("frame"))
    out = [blocks[0]]
    for d in range(1, group):
        out.append(lax.ppermute(blocks[d], "frame", [(i, i ^ d) for i in devices]))
    return out


def shifted(block, axis, distance):
    devices = range(lax.axis_size(axis))
    route = [(i - distance, i) for i in devices if i - distance in devices]
    return lax.ppermute(block, axis, route)


def doubled(total, axis, bit):
    devices = range(lax.axis_size(axis))
    return total + lax.ppermute(total, axis, [(i, i ^ bit) for i in devices])


def total_of_all(totals, group):
    sizes = [lax.axis_size("row"), lax.axis_size("frame")]
    if any(size & (size - 1) for size in sizes):
        return lax.psum(totals, ("frame", "row"))
    bit = 1
    while bit < sizes[0]:
        totals = doubled(totals, "row", bit)
        bit *= 2
    bit = group
    while bit < sizes[1]:
        totals = doubled(totals, "frame", bit)
        bit *= 2
    parts = swap([totals] * group, group)
    while len(parts) > 1:
        parts = [parts[k] + parts[k + 1] for k in range(0, len(parts), 2)]
    return parts[0]


def shards(footage):
    frames, rows, width = footage.shape
    group = SPAN // frames
    strips = strips_of(rows)
    weights = jnp.asarray(np.stack([column_weights(2**level) for level in range(SLEVELS)]))
    top = shifted(footage[:, rows - HALO :], "row", 1)
    bottom = shifted(footage[:, :HALO], "row", -1)
    sent, arrived, chosen = [[], []], [[], []], [[], []]
    for u, (which, own) in enumerate(UNITS):
        pieces = space(u, footage, top, bottom, weights, strips, group)
        sent[which].append(pieces)
        chosen[which].append(own)
        arrived[which] += swap(pieces, group)
    coeffs = None
    for which, strip in enumerate(strips):
        coeffs = home(group, strip, chosen[which], sent[which], footage.shape, coeffs)
    power = None
    back = []
    turns = turns_of(strips, group)
    for which, first, count in turns:
        given, own = arrived[which], chosen[which]
        to_right, to_left = edges(group, first, count, own, given)
        left = shifted(to_right, "frame", group)
        right = shifted(to_left, "frame", -group)
        pieces, part_power = finish_time(group, first, count, own, given, left, right)
        back.append(swap(pieces, group))
        power = part_power if power is None else power + part_power
    period = 2**SLEVELS
    column_phase = np.arange(width) % period
    selector = jnp.asarray((column_phase[:, None] == np.arange(period)[None, :]).astype(np.float32))
    pattern = jnp.dot(
        power.reshape((TLEVELS + 1) * SUB, width), selector, precision=lax.Precision.HIGHEST
    ).reshape(TLEVELS + 1, SUB * period)
    totals = jnp.dot(
        pattern, jnp.asarray(space_table(SLEVELS), jnp.float32), precision=lax.Precision.HIGHEST
    )
    totals = total_of_all(totals, group)
    for t, (which, first, _) in enumerate(turns):
        coeffs = place(group, strips[which], first, back[t], coeffs)
    means = band_means(
        totals,
        frames * lax.axis_size("frame"),
        rows * lax.axis_size("row"),
        width,
        SLEVELS,
        TLEVELS,
    )
    return (coeffs, means)


def solution(mesh):
    return jax.shard_map(
        shards,
        mesh=mesh,
        in_specs=(P("frame", "row", None),),
        out_specs=(P("frame", "row", None), P()),
        check_vma=False,
    )
```

time: 298 us -> 239 us (0.80)
  waiting for transfers between devices: 145 us -> 68.5 us
  starting transfers between devices: 34.3 us -> 60.2 us
  Pallas kernels: 106 us -> 93 us
  local copies, waits for them, and re-layouts: 5.15 us -> 9.57 us
    ppermute x18 -> x27, waiting for transfers between devices: 126 us -> 62.2 us  [swap(): out.append(lax.ppermute(blocks[d], 'frame', [(i, i ^ d) for i in devices]))]
    ppermute x18 -> x27, starting transfers between devices: 17.9 us -> 34 us  [swap(): out.append(lax.ppermute(blocks[d], 'frame', [(i, i ^ d) for i in devices]))]
    pallas_call x8 -> x16, Pallas kernels: 106 us -> 93 us  [the longest x5 57.8 us: space(): pl.pallas_call(functools.partial(space_kernel, group, strip, rows), grid=...]
    ppermute x6 -> x8, waiting for transfers between devices: 12.5 us -> 0.02 us  [shifted(): return lax.ppermute(block, axis, route)]
    ppermute x6 -> x8, starting transfers between devices: 15 us -> 22.9 us  [shifted(): return lax.ppermute(block, axis, route)]
    unnamed x36 -> x62, local copies, waits for them, and re-layouts: 3.77 us -> 7.17 us
  transfers between devices with their start and end apart: 27 -> 38, of which waited for: 15 -> 11; matrix products, arithmetic and copies ran while one was open for 1% -> 1% of each run, Pallas kernels for 28% -> 39%
where the time goes in v2:
time: 239 us; the launch traced here: 235 us
  Pallas kernels  93 us (39%)
  waiting for transfers between devices  68.5 us (29%)
  starting transfers between devices  60.2 us (25%)
  local copies, waits for them, and re-layouts  9.57 us (4%)
    ppermute x27, waiting for transfers between devices, swap(): out.append(lax.ppermute(blocks[d], 'frame', [(i, i ^ d) for i in devices]))  62.2 us
    pallas_call x5, Pallas kernels, space(): pl.pallas_call(functools.partial(space_kernel, group, strip, rows), grid=...  57.8 us
    ppermute x27, starting transfers between devices, swap(): out.append(lax.ppermute(blocks[d], 'frame', [(i, i ^ d) for i in devices]))  34 us
    ppermute x8, starting transfers between devices, shifted(): return lax.ppermute(block, axis, route)  22.9 us
    pallas_call x3, Pallas kernels, finish_time(): pl.pallas_call(functools.partial(time_kernel, group, chosen), grid=(rows...  12.5 us
    pallas_call x3, Pallas kernels, edges(): pl.pallas_call(functools.partial(edges_kernel, group, chosen), grid=(rows...  9.59 us
    pallas_call x3, Pallas kernels, place(): pl.pallas_call(functools.partial(place_kernel, group, strip, first), in_s...  7.46 us
    unnamed x62, local copies, waits for them, and re-layouts  7.17 us
  transfers between devices with their start and end apart: 38, of which 11 were waited for; matrix products, arithmetic and copies ran while one was open for 1% of the time, Pallas kernels for 39%

profile of v2, /device:TPU:14, one launch (start us, length us, event | category | flops | bytes accessed | tf_op | source)
XLA Modules:
  0.0 235.2 jit_solution(4786289249618587547)
XLA Ops:
  0.6 2.3 fusion.1
  2.9 1.3 collective-permute-start.1
  4.2 3.1 %collective-permute-start = (f32[4,32,1024]{2,1,0:T(8,128)}, f32[4,32,1024]{2,1,0:T(8,128)S(1)}, u32[]{:S(2)}, u32[]{:S(2)}) collective-permute-start(f32[4,32,1024]{2,1,0:T(8,128)} %get-tuple-element.85), channel_id=1, source_target_pairs={{0,1},{2,3},{4,5},{6,7},{8,9},{10,11},{12,13},{14,15},{16,17},{18,... | collective-permute-start | bytes 1572872 | tf_op jit(solution)/shard_map/ppermute | solution.py:626
  7.3 7.7 %shard_map.74 = (f32[1,64,1024]{2,1,0:T(8,128)}, f32[1,64,1024]{2,1,0:T(8,128)}, f32[1,64,1024]{2,1,0:T(8,128)}, f32[1,64,1024]{2,1,0:T(8,128)}) custom-call(f32[4,512,1024]{2,1,0:T(8,128)} %refs_0_.9, bf16[3,1024,256]{2,1,0:T(8,128)(2,1)} %constant.8.clone.refs_3_.refs_1_), custom_call_target="tpu_custom_call" | custom-call | flops 209715200 | bytes 4194304 | tf_op jit(solution)/shard_map/pallas_call | solution.py:327
  16.1 12.5 %shard_map.76 = (f32[2,64,1024]{2,1,0:T(8,128)}, f32[2,64,1024]{2,1,0:T(8,128)}, f32[2,64,1024]{2,1,0:T(8,128)}, f32[2,64,1024]{2,1,0:T(8,128)}) custom-call(f32[4,512,1024]{2,1,0:T(8,128)} %refs_0_.9, bf16[3,1024,256]{2,1,0:T(8,128)(2,1)} %constant.8.clone.refs_3_.refs_1_), custom_call_target="tpu_custom_call" | custom-call | flops 419430400 | bytes 8388608 | tf_op jit(solution)/shard_map/pallas_call | solution.py:327
  28.5 1.5 collective-permute-start.24
  30.0 7.7 %shard_map.75 = (f32[1,64,1024]{2,1,0:T(8,128)}, f32[1,64,1024]{2,1,0:T(8,128)}, f32[1,64,1024]{2,1,0:T(8,128)}, f32[1,64,1024]{2,1,0:T(8,128)}) custom-call(f32[4,512,1024]{2,1,0:T(8,128)} %refs_0_.9, bf16[3,1024,256]{2,1,0:T(8,128)(2,1)} %constant.8.clone.refs_3_.refs_1_), custom_call_target="tpu_custom_call" | custom-call | flops 209715200 | bytes 4194304 | tf_op jit(solution)/shard_map/pallas_call | solution.py:327
  37.8 1.6 collective-permute-start.20
  39.3 1.5 collective-permute-start.21
  41.3 1.5 collective-permute-start.23
  42.8 14.9 %shard_map.69 = (f32[2,64,1024]{2,1,0:T(8,128)}, f32[2,64,1024]{2,1,0:T(8,128)}, f32[2,64,1024]{2,1,0:T(8,128)}, f32[2,64,1024]{2,1,0:T(8,128)}) custom-call(f32[4,512,1024]{2,1,0:T(8,128)} %refs_0_.9, f32[4,32,1024]{2,1,0:T(8,128)} %copy-done.10, f32[4,32,1024]{2,1,0:T(8,128)} %copy-done.9, bf16[3,1024,256]{2,1,0:T(8,128)(2,1)} %constant.8.clone.refs_3_.refs_1_), custom_call_target="tpu_custom_call" | custom-call | flops 419430400 | bytes 8388608 | tf_op jit(solution)/shard_map/pallas_call | solution.py:327
  57.8 0.9 collective-permute-start.25
  59.4 2.1 collective-permute-start.26
  62.1 0.9 collective-permute-start.6
  63.0 0.8 copy-done.6
  63.8 2.1 collective-permute-start.7
  65.9 14.9 %shard_map.68 = (f32[2,64,1024]{2,1,0:T(8,128)}, f32[2,64,1024]{2,1,0:T(8,128)}, f32[2,64,1024]{2,1,0:T(8,128)}, f32[2,64,1024]{2,1,0:T(8,128)}) custom-call(f32[4,512,1024]{2,1,0:T(8,128)} %refs_0_.9, f32[4,32,1024]{2,1,0:T(8,128)} %copy-done.10, f32[4,32,1024]{2,1,0:T(8,128)} %copy-done.9, bf16[3,1024,256]{2,1,0:T(8,128)(2,1)} %constant.8.clone.refs_3_.refs_1_), custom_call_target="tpu_custom_call" | custom-call | flops 419430400 | bytes 8388608 | tf_op jit(solution)/shard_map/pallas_call | solution.py:327
  80.9 5.7 %collective-permute-done.25.refs_10_ = f32[2,64,1024]{2,1,0:T(8,128)S(1)} collective-permute-done((f32[2,64,1024]{2,1,0:T(8,128)S(1)}, f32[2,64,1024]{2,1,0:T(8,128)S(1)}, u32[]{:S(2)}, u32[]{:S(2)}) %collective-permute-start.25) | collective-permute-done | bytes 524320 | tf_op jit(solution)/shard_map/ppermute | solution.py:619
  86.6 0.8 copy-done.7
  87.4 1.2 collective-permute-start.2
  88.6 0.8 copy-done.8
  89.4 1.5 collective-permute-start.3
  90.9 0.8 collective-permute-start.4
  91.7 3.7 %shard_map.77 = (f32[3,64,1024]{2,1,0:T(8,128)}, f32[3,64,1024]{2,1,0:T(8,128)}) custom-call(f32[1,64,1024]{2,1,0:T(8,128)} %get-tuple-element.63.refs_0_, f32[1,64,1024]{2,1,0:T(8,128)} %copy-done.11, f32[1,64,1024]{2,1,0:T(8,128)} %copy-done.12, f32[1,64,1024]{2,1,0:T(8,128)} %copy-done.13, f32[1,64,1024]{2,1,0:T(8,128)} %get-tuple-element.67.refs_4_, ...), custom_call_target="tpu_custom_call" | custom-call | flops 131072000 | bytes 5767168 | tf_op jit(solution)/shard_map/pallas_call | solution.py:493
  95.4 13.6 %collective-permute-done.6.refs_6_ = f32[2,64,1024]{2,1,0:T(8,128)S(1)} collective-permute-done((f32[2,64,1024]{2,1,0:T(8,128)}, f32[2,64,1024]{2,1,0:T(8,128)S(1)}, u32[]{:S(2)}, u32[]{:S(2)}) %collective-permute-start.6) | collective-permute-done | bytes 524320 | tf_op jit(solution)/shard_map/ppermute | solution.py:619
  109.1 3.5 %collective-permute-start.27 = (f32[3,64,1024]{2,1,0:T(8,128)}, f32[3,64,1024]{2,1,0:T(8,128)}, u32[]{:S(2)}, u32[]{:S(2)}) collective-permute-start(f32[3,64,1024]{2,1,0:T(8,128)} %get-tuple-element.75), channel_id=1, source_target_pairs={{0,8},{2,10},{4,12},{6,14},{8,16},{10,18},{12,20},{14,22},{16,24},... | collective-permute-start | bytes 2359304 | tf_op jit(solution)/shard_map/ppermute | solution.py:626
  112.6 3.2 %collective-permute-start.28 = (f32[3,64,1024]{2,1,0:T(8,128)}, f32[3,64,1024]{2,1,0:T(8,128)}, u32[]{:S(2)}, u32[]{:S(2)}) collective-permute-start(f32[3,64,1024]{2,1,0:T(8,128)} %get-tuple-element.76), channel_id=1, source_target_pairs={{8,0},{10,2},{12,4},{14,6},{16,8},{18,10},{20,12},{22,14},{24,16},... | collective-permute-start | bytes 2359304 | tf_op jit(solution)/shard_map/ppermute | solution.py:626
  115.8 10.8 %collective-permute-done.3.refs_2_ = f32[2,64,1024]{2,1,0:T(8,128)S(1)} collective-permute-done((f32[2,64,1024]{2,1,0:T(8,128)}, f32[2,64,1024]{2,1,0:T(8,128)S(1)}, u32[]{:S(2)}, u32[]{:S(2)}) %collective-permute-start.3) | collective-permute-done | bytes 524320 | tf_op jit(solution)/shard_map/ppermute | solution.py:619
  127.6 2.9 %shard_map.72 = (f32[3,32,1024]{2,1,0:T(8,128)}, f32[3,32,1024]{2,1,0:T(8,128)}) custom-call(f32[2,64,1024]{2,1,0:T(8,128)} %get-tuple-element.43.refs_0_.refs_4_, f32[2,64,1024]{2,1,0:T(8,128)} %copy-done.3, f32[2,64,1024]{2,1,0:T(8,128)} %copy-done.4, f32[2,64,1024]{2,1,0:T(8,128)} %copy-done.5, f32[2,64,1024]{2,1,0:T(8,128)} %get-tuple-element.47.refs_4_.refs_8_, ...), custom_call_target="tpu_custom_call" | custom-call | flops 65536000 | bytes 2883584 | tf_op jit(solution)/shard_map/pallas_call | solution.py:493
  130.5 3.5 %collective-permute-start.13 = (f32[3,32,1024]{2,1,0:T(8,128)}, f32[3,32,1024]{2,1,0:T(8,128)S(1)}, u32[]{:S(2)}, u32[]{:S(2)}) collective-permute-start(f32[3,32,1024]{2,1,0:T(8,128)} %get-tuple-element.57), channel_id=1, source_target_pairs={{0,8},{2,10},{4,12},{6,14},{8,16},{10,18},{12,20},{14,22},{16,24},... | collective-permute-start | bytes 1179656 | tf_op jit(solution)/shard_map/ppermute | solution.py:626
  134.0 2.4 %collective-permute-start.14 = (f32[3,32,1024]{2,1,0:T(8,128)}, f32[3,32,1024]{2,1,0:T(8,128)S(1)}, u32[]{:S(2)}, u32[]{:S(2)}) collective-permute-start(f32[3,32,1024]{2,1,0:T(8,128)} %get-tuple-element.58), channel_id=1, source_target_pairs={{8,0},{10,2},{12,4},{14,6},{16,8},{18,10},{20,12},{22,14},{24,16},... | collective-permute-start | bytes 1179656 | tf_op jit(solution)/shard_map/ppermute | solution.py:626
  136.4 3.0 %shard_map.70 = (f32[3,32,1024]{2,1,0:T(8,128)}, f32[3,32,1024]{2,1,0:T(8,128)}) custom-call(f32[2,64,1024]{2,1,0:T(8,128)} %get-tuple-element.43.refs_0_.refs_4_, f32[2,64,1024]{2,1,0:T(8,128)} %copy-done.3, f32[2,64,1024]{2,1,0:T(8,128)} %copy-done.4, f32[2,64,1024]{2,1,0:T(8,128)} %copy-done.5, f32[2,64,1024]{2,1,0:T(8,128)} %get-tuple-element.47.refs_4_.refs_8_, ...), custom_call_target="tpu_custom_call" | custom-call | flops 65536000 | bytes 2883584 | tf_op jit(solution)/shard_map/pallas_call | solution.py:493
  139.4 3.6 %collective-permute-start.8 = (f32[3,32,1024]{2,1,0:T(8,128)}, f32[3,32,1024]{2,1,0:T(8,128)S(1)}, u32[]{:S(2)}, u32[]{:S(2)}) collective-permute-start(f32[3,32,1024]{2,1,0:T(8,128)} %get-tuple-element.51), channel_id=1, source_target_pairs={{0,8},{2,10},{4,12},{6,14},{8,16},{10,18},{12,20},{14,22},{16,24},... | collective-permute-start | bytes 1179656 | tf_op jit(solution)/shard_map/ppermute | solution.py:626
  143.0 2.4 %collective-permute-start.9 = (f32[3,32,1024]{2,1,0:T(8,128)}, f32[3,32,1024]{2,1,0:T(8,128)}, u32[]{:S(2)}, u32[]{:S(2)}) collective-permute-start(f32[3,32,1024]{2,1,0:T(8,128)} %get-tuple-element.52), channel_id=1, source_target_pairs={{8,0},{10,2},{12,4},{14,6},{16,8},{18,10},{20,12},{22,14},{24,16},... | collective-permute-start | bytes 1179656 | tf_op jit(solution)/shard_map/ppermute | solution.py:626
  145.4 4.9 %shard_map.78 = (f32[3,64,1024]{2,1,0:T(8,128)}, f32[3,64,1024]{2,1,0:T(8,128)}, f32[3,64,1024]{2,1,0:T(8,128)}, f32[3,64,1024]{2,1,0:T(8,128)}, f32[4,8,1024]{2,1,0:T(8,128)}) custom-call(f32[1,64,1024]{2,1,0:T(8,128)} %get-tuple-element.63.refs_0_, f32[1,64,1024]{2,1,0:T(8,128)} %copy-done.11, f32[1,64,1024]{2,1,0:T(8,128)} %copy-done.12, ...), custom_call_target="tpu_custom_call" | custom-call | flops 131072000 | bytes 9961472 | tf_op jit(solution)/shard_map/pallas_call | solution.py:507
  150.3 1.6 collective-permute-start.29
  151.9 0.7 copy-done.21
  153.2 0.8 copy-done.22
  153.9 1.5 collective-permute-start.31
  155.4 3.8 %shard_map.73 = (f32[3,32,1024]{2,1,0:T(8,128)}, f32[3,32,1024]{2,1,0:T(8,128)}, f32[3,32,1024]{2,1,0:T(8,128)}, f32[3,32,1024]{2,1,0:T(8,128)}, f32[4,8,1024]{2,1,0:T(8,128)}) custom-call(f32[2,64,1024]{2,1,0:T(8,128)} %get-tuple-element.43.refs_0_.refs_4_, f32[2,64,1024]{2,1,0:T(8,128)} %copy-done.3, f32[2,64,1024]{2,1,0:T(8,128)} %copy-done.4, ...), custom_call_target="tpu_custom_call" | custom-call | flops 65536000 | bytes 4980736 | tf_op jit(solution)/shard_map/pallas_call | solution.py:507
  159.2 1.6 collective-permute-start.15
  160.8 3.8 %shard_map.71 = (f32[3,32,1024]{2,1,0:T(8,128)}, f32[3,32,1024]{2,1,0:T(8,128)}, f32[3,32,1024]{2,1,0:T(8,128)}, f32[3,32,1024]{2,1,0:T(8,128)}, f32[4,8,1024]{2,1,0:T(8,128)}) custom-call(f32[2,64,1024]{2,1,0:T(8,128)} %get-tuple-element.43.refs_0_.refs_4_, f32[2,64,1024]{2,1,0:T(8,128)} %copy-done.3, f32[2,64,1024]{2,1,0:T(8,128)} %copy-done.4, ...), custom_call_target="tpu_custom_call" | custom-call | flops 65536000 | bytes 4980736 | tf_op jit(solution)/shard_map/pallas_call | solution.py:507
  164.6 1.4 fusion
  166.2 1.2 collective-permute-done.32
  167.4 3.6 %collective-permute-done.33 = f32[4,10]{1,0:T(4,128)S(1)} collective-permute-done((f32[4,10]{1,0:T(4,128)S(1)}, f32[4,10]{1,0:T(4,128)S(1)}, u32[]{:S(2)}, u32[]{:S(2)}) %collective-permute-start.33) | collective-permute-done | bytes 192 | tf_op jit(solution)/shard_map/ppermute | solution.py:631
  171.0 3.3 %collective-permute-start.34 = (f32[4,10]{1,0:T(4,128)S(1)}, f32[4,10]{1,0:T(4,128)S(1)}, u32[]{:S(2)}, u32[]{:S(2)}) collective-permute-start(f32[4,10]{1,0:T(4,128)S(1)} %add.27), channel_id=1, source_target_pairs={{0,16},{2,18},{4,20},{6,22},{8,24},{10,26},{12,28},{14,30},{16,0},... | collective-permute-start | bytes 488 | tf_op jit(solution)/shard_map/ppermute | solution.py:631
  174.3 1.6 collective-permute-done.34
  176.5 16.2 %collective-permute-done.37 = f32[4,10]{1,0:T(4,128)S(1)} collective-permute-done((f32[4,10]{1,0:T(4,128)S(1)}, f32[4,10]{1,0:T(4,128)S(1)}, u32[]{:S(2)}, u32[]{:S(2)}) %collective-permute-start.37) | collective-permute-done | bytes 192 | tf_op jit(solution)/shard_map/ppermute | solution.py:619
  192.7 2.2 collective-permute-start.36
  194.9 1.6 collective-permute-done.36
  196.4 1.7 collective-permute-start.35
  198.1 1.9 collective-permute-done.35
  200.1 2.1 collective-permute-start.16
  202.1 1.2 collective-permute-start.17
  203.9 1.8 collective-permute-start.11
  205.6 1.2 collective-permute-start.12
  206.8 2.8 %shard_map.79.refs_12_ = f32[4,512,1024]{2,1,0:T(8,128)} custom-call(f32[1,64,1024]{2,1,0:T(8,128)} %get-tuple-element.63.refs_0_, f32[1,64,1024]{2,1,0:T(8,128)} %get-tuple-element.64.refs_1_, f32[1,64,1024]{2,1,0:T(8,128)} %get-tuple-element.65.refs_2_, f32[1,64,1024]{2,1,0:T(8,128)} %get-tuple-element.66.refs_3_, ...), custom_call_target="tpu_custom_call" | custom-call | flops 131072000 | bytes 4194304 | tf_op jit(solution)/shard_map/pallas_call | solution.py:559
  209.6 2.8 %shard_map.80.refs_4_ = f32[4,512,1024]{2,1,0:T(8,128)} custom-call(f32[2,64,1024]{2,1,0:T(8,128)} %get-tuple-element.43.refs_0_.refs_4_, f32[2,64,1024]{2,1,0:T(8,128)} %get-tuple-element.44.refs_1_.refs_5_, f32[2,64,1024]{2,1,0:T(8,128)} %get-tuple-element.45.refs_2_.refs_6_, ...), custom_call_target="tpu_custom_call", output_to_operand_aliasing={{}: (12, {})} | custom-call | flops 131072000 | bytes 4194304 | tf_op jit(solution)/shard_map/pallas_call | solution.py:559
  212.5 1.3 add_multiply_fusion
  213.8 2.8 %shard_map.81.refs_4_ = f32[4,512,1024]{2,1,0:T(8,128)} custom-call(f32[3,64,1024]{2,1,0:T(8,128)} %get-tuple-element.77.refs_0_, f32[3,64,1024]{2,1,0:T(8,128)} %copy-done.15, f32[3,64,1024]{2,1,0:T(8,128)} %copy-done.16, f32[3,64,1024]{2,1,0:T(8,128)} %copy-done.17, f32[4,512,1024]{2,1,0:T(8,128)} %shard_map.80.refs_4_), custom_call_target="tpu_custom_call", output_to_operand_aliasing={{}: (4, {})} | custom-call | flops 131072000 | bytes 6291456 | tf_op jit(solution)/shard_map/pallas_call | solution.py:600
  216.6 7.8 %collective-permute-done.16.refs_2_ = f32[3,32,1024]{2,1,0:T(8,128)S(1)} collective-permute-done((f32[3,32,1024]{2,1,0:T(8,128)}, f32[3,32,1024]{2,1,0:T(8,128)S(1)}, u32[]{:S(2)}, u32[]{:S(2)}) %collective-permute-start.16) | collective-permute-done | bytes 393248 | tf_op jit(solution)/shard_map/ppermute | solution.py:619
  225.2 2.3 shard_map.82.refs_4_
  227.5 4.4 %collective-permute-done.11.refs_2_ = f32[3,32,1024]{2,1,0:T(8,128)S(1)} collective-permute-done((f32[3,32,1024]{2,1,0:T(8,128)}, f32[3,32,1024]{2,1,0:T(8,128)S(1)}, u32[]{:S(2)}, u32[]{:S(2)}) %collective-permute-start.11) | collective-permute-done | bytes 393248 | tf_op jit(solution)/shard_map/ppermute | solution.py:619
  232.7 2.3 shard_map.83
  (98 shorter events, 7.3 us)
Async XLA Ops:
  2.9 37.9 %collective-permute-start.1 = (f32[4,32,1024]{2,1,0:T(8,128)}, f32[4,32,1024]{2,1,0:T(8,128)S(1)}, u32[]{:S(2)}, u32[]{:S(2)}) collective-permute-start(f32[4,32,1024]{2,1,0:T(8,128)} %get-tuple-element.84), channel_id=1, source_target_pairs={{1,0},{3,2},{5,4},{7,6},{9,8},{11,10},{13,12},{15,14},{17,16},{19,... | collective-permute-start | bytes 1572872 | tf_op jit(solution)/shard_map/ppermute | solution.py:626
  4.2 37.1 %collective-permute-start = (f32[4,32,1024]{2,1,0:T(8,128)}, f32[4,32,1024]{2,1,0:T(8,128)S(1)}, u32[]{:S(2)}, u32[]{:S(2)}) collective-permute-start(f32[4,32,1024]{2,1,0:T(8,128)} %get-tuple-element.85), channel_id=1, source_target_pairs={{0,1},{2,3},{4,5},{6,7},{8,9},{10,11},{12,13},{14,15},{16,17},{18,... | collective-permute-start | bytes 1572872 | tf_op jit(solution)/shard_map/ppermute | solution.py:626
  15.0 22.7 %collective-permute-start.18 = (f32[1,64,1024]{2,1,0:T(8,128)}, f32[1,64,1024]{2,1,0:T(8,128)S(1)}, u32[]{:S(2)}, u32[]{:S(2)}) collective-permute-start(f32[1,64,1024]{2,1,0:T(8,128)} %get-tuple-element.64.refs_1_), channel_id=1, source_target_pairs={{0,2},{2,0},{4,6},{6,4},{8,10},{10,8},{12,14},{14,12},{16,18},{18,... | collective-permute-start | bytes 786440 | tf_op jit(solution)/shard_map/ppermute | solution.py:619
  15.6 22.2 %copy-start.26 = (f32[1,64,1024]{2,1,0:T(8,128)S(1)}, f32[1,64,1024]{2,1,0:T(8,128)}, u32[]{:S(2)}) copy-start(f32[1,64,1024]{2,1,0:T(8,128)} %get-tuple-element.66.refs_3_) | copy-start | bytes 786436
  15.6 23.8 %collective-permute-start.19 = (f32[1,64,1024]{2,1,0:T(8,128)}, f32[1,64,1024]{2,1,0:T(8,128)S(1)}, u32[]{:S(2)}, u32[]{:S(2)}) collective-permute-start(f32[1,64,1024]{2,1,0:T(8,128)} %get-tuple-element.65.refs_2_), channel_id=1, source_target_pairs={{0,4},{2,6},{4,0},{6,2},{8,12},{10,14},{12,8},{14,10},{16,20},{18,... | collective-permute-start | bytes 786440 | tf_op jit(solution)/shard_map/ppermute | solution.py:619
  28.5 29.2 %copy-start.18 = (f32[2,64,1024]{2,1,0:T(8,128)S(1)}, f32[2,64,1024]{2,1,0:T(8,128)}, u32[]{:S(2)}) copy-start(f32[2,64,1024]{2,1,0:T(8,128)} %get-tuple-element.73.refs_10_) | copy-start | bytes 1572868
  28.5 34.4 %collective-permute-start.24 = (f32[2,64,1024]{2,1,0:T(8,128)}, f32[2,64,1024]{2,1,0:T(8,128)S(1)}, u32[]{:S(2)}, u32[]{:S(2)}) collective-permute-start(f32[2,64,1024]{2,1,0:T(8,128)} %get-tuple-element.72.refs_9_), channel_id=1, source_target_pairs={{0,2},{2,0},{4,6},{6,4},{8,10},{10,8},{12,14},{14,12},{16,18},{18,... | collective-permute-start | bytes 1572872 | tf_op jit(solution)/shard_map/ppermute | solution.py:619
  37.8 54.0 %copy-start.11 = (f32[1,64,1024]{2,1,0:T(8,128)}, f32[1,64,1024]{2,1,0:T(8,128)S(1)}, u32[]{:S(2)}) copy-start(f32[1,64,1024]{2,1,0:T(8,128)S(1)} %collective-permute-done.18.refs_1_) | copy-start | bytes 786436
  37.8 20.0 %collective-permute-start.20 = (f32[1,64,1024]{2,1,0:T(8,128)S(1)}, f32[1,64,1024]{2,1,0:T(8,128)S(1)}, u32[]{:S(2)}, u32[]{:S(2)}) collective-permute-start(f32[1,64,1024]{2,1,0:T(8,128)S(1)} %copy-done.26), channel_id=1, source_target_pairs={{0,6},{2,4},{4,2},{6,0},{8,14},{10,12},{12,10},{14,8},{16,22},{18,... | collective-permute-start | bytes 786440 | tf_op jit(solution)/shard_map/ppermute | solution.py:619
  39.3 22.8 %copy-start.12 = (f32[1,64,1024]{2,1,0:T(8,128)}, f32[1,64,1024]{2,1,0:T(8,128)S(1)}, u32[]{:S(2)}) copy-start(f32[1,64,1024]{2,1,0:T(8,128)S(1)} %collective-permute-done.19.refs_2_) | copy-start | bytes 786436
  39.3 19.3 %collective-permute-start.21 = (f32[1,64,1024]{2,1,0:T(8,128)}, f32[1,64,1024]{2,1,0:T(8,128)S(1)}, u32[]{:S(2)}, u32[]{:S(2)}) collective-permute-start(f32[1,64,1024]{2,1,0:T(8,128)} %get-tuple-element.68.refs_5_), channel_id=1, source_target_pairs={{0,2},{2,0},{4,6},{6,4},{8,10},{10,8},{12,14},{14,12},{16,18},{18,... | collective-permute-start | bytes 786440 | tf_op jit(solution)/shard_map/ppermute | solution.py:619
  40.8 2.0 copy-start.9
  40.8 20.7 %collective-permute-start.22 = (f32[1,64,1024]{2,1,0:T(8,128)}, f32[1,64,1024]{2,1,0:T(8,128)}, u32[]{:S(2)}, u32[]{:S(2)}) collective-permute-start(f32[1,64,1024]{2,1,0:T(8,128)} %get-tuple-element.69.refs_6_), channel_id=1, source_target_pairs={{0,4},{2,6},{4,0},{6,2},{8,12},{10,14},{12,8},{14,10},{16,20},{18,... | collective-permute-start | bytes 786440 | tf_op jit(solution)/shard_map/ppermute | solution.py:619
  41.3 1.5 copy-start.10
  41.3 20.7 %collective-permute-start.23 = (f32[1,64,1024]{2,1,0:T(8,128)}, f32[1,64,1024]{2,1,0:T(8,128)}, u32[]{:S(2)}, u32[]{:S(2)}) collective-permute-start(f32[1,64,1024]{2,1,0:T(8,128)} %get-tuple-element.70.refs_7_), channel_id=1, source_target_pairs={{0,6},{2,4},{4,2},{6,0},{8,14},{10,12},{12,10},{14,8},{16,22},{18,... | collective-permute-start | bytes 786440 | tf_op jit(solution)/shard_map/ppermute | solution.py:619
  57.8 4.3 %copy-start.13 = (f32[1,64,1024]{2,1,0:T(8,128)}, f32[1,64,1024]{2,1,0:T(8,128)S(1)}, u32[]{:S(2)}) copy-start(f32[1,64,1024]{2,1,0:T(8,128)S(1)} %collective-permute-done.20.refs_3_) | copy-start | bytes 786436
  57.8 28.8 %collective-permute-start.25 = (f32[2,64,1024]{2,1,0:T(8,128)S(1)}, f32[2,64,1024]{2,1,0:T(8,128)S(1)}, u32[]{:S(2)}, u32[]{:S(2)}) collective-permute-start(f32[2,64,1024]{2,1,0:T(8,128)S(1)} %copy-done.18), channel_id=1, source_target_pairs={{0,4},{2,6},{4,0},{6,2},{8,12},{10,14},{12,8},{14,10},{16,20},{18,... | collective-permute-start | bytes 1572872 | tf_op jit(solution)/shard_map/ppermute | solution.py:619
  59.4 29.2 %collective-permute-start.26 = (f32[2,64,1024]{2,1,0:T(8,128)}, f32[2,64,1024]{2,1,0:T(8,128)S(1)}, u32[]{:S(2)}, u32[]{:S(2)}) collective-permute-start(f32[2,64,1024]{2,1,0:T(8,128)} %get-tuple-element.74.refs_11_), channel_id=1, source_target_pairs={{0,6},{2,4},{4,2},{6,0},{8,14},{10,12},{12,10},{14,8},{16,22},{18,... | collective-permute-start | bytes 1572872 | tf_op jit(solution)/shard_map/ppermute | solution.py:619
  61.5 29.4 %collective-permute-start.5 = (f32[2,64,1024]{2,1,0:T(8,128)}, f32[2,64,1024]{2,1,0:T(8,128)S(1)}, u32[]{:S(2)}, u32[]{:S(2)}) collective-permute-start(f32[2,64,1024]{2,1,0:T(8,128)} %get-tuple-element.48.refs_9_), channel_id=1, source_target_pairs={{0,2},{2,0},{4,6},{6,4},{8,10},{10,8},{12,14},{14,12},{16,18},{18,... | collective-permute-start | bytes 1572872 | tf_op jit(solution)/shard_map/ppermute | solution.py:619
  62.1 47.0 %collective-permute-start.6 = (f32[2,64,1024]{2,1,0:T(8,128)}, f32[2,64,1024]{2,1,0:T(8,128)S(1)}, u32[]{:S(2)}, u32[]{:S(2)}) collective-permute-start(f32[2,64,1024]{2,1,0:T(8,128)} %get-tuple-element.49.refs_10_), channel_id=1, source_target_pairs={{0,4},{2,6},{4,0},{6,2},{8,12},{10,14},{12,8},{14,10},{16,20},{18,... | collective-permute-start | bytes 1572872 | tf_op jit(solution)/shard_map/ppermute | solution.py:619
  63.0 0.8 copy-start.6
  63.8 48.8 %collective-permute-start.7 = (f32[2,64,1024]{2,1,0:T(8,128)}, f32[2,64,1024]{2,1,0:T(8,128)S(1)}, u32[]{:S(2)}, u32[]{:S(2)}) collective-permute-start(f32[2,64,1024]{2,1,0:T(8,128)} %get-tuple-element.50.refs_11_), channel_id=1, source_target_pairs={{0,6},{2,4},{4,2},{6,0},{8,14},{10,12},{12,10},{14,8},{16,22},{18,... | collective-permute-start | bytes 1572872 | tf_op jit(solution)/shard_map/ppermute | solution.py:619
  86.6 0.8 copy-start.7
  87.4 28.4 %collective-permute-start.2 = (f32[2,64,1024]{2,1,0:T(8,128)}, f32[2,64,1024]{2,1,0:T(8,128)S(1)}, u32[]{:S(2)}, u32[]{:S(2)}) collective-permute-start(f32[2,64,1024]{2,1,0:T(8,128)} %get-tuple-element.44.refs_1_.refs_5_), channel_id=1, source_target_pairs={{0,2},{2,0},{4,6},{6,4},{8,10},{10,8},{12,14},{14,12},{16,18},{18,... | collective-permute-start | bytes 1572872 | tf_op jit(solution)/shard_map/ppermute | solution.py:619
  88.6 0.8 copy-start.8
  89.4 37.2 %collective-permute-start.3 = (f32[2,64,1024]{2,1,0:T(8,128)}, f32[2,64,1024]{2,1,0:T(8,128)S(1)}, u32[]{:S(2)}, u32[]{:S(2)}) collective-permute-start(f32[2,64,1024]{2,1,0:T(8,128)} %get-tuple-element.45.refs_2_.refs_6_), channel_id=1, source_target_pairs={{0,4},{2,6},{4,0},{6,2},{8,12},{10,14},{12,8},{14,10},{16,20},{18,... | collective-permute-start | bytes 1572872 | tf_op jit(solution)/shard_map/ppermute | solution.py:619
  90.9 35.7 %copy-start = (f32[2,64,1024]{2,1,0:T(8,128)}, f32[2,64,1024]{2,1,0:T(8,128)S(1)}, u32[]{:S(2)}) copy-start(f32[2,64,1024]{2,1,0:T(8,128)S(1)} %collective-permute-done.5.refs_5_) | copy-start | bytes 1572868
  90.9 35.7 %collective-permute-start.4 = (f32[2,64,1024]{2,1,0:T(8,128)}, f32[2,64,1024]{2,1,0:T(8,128)S(1)}, u32[]{:S(2)}, u32[]{:S(2)}) collective-permute-start(f32[2,64,1024]{2,1,0:T(8,128)} %get-tuple-element.46.refs_3_.refs_7_), channel_id=1, source_target_pairs={{0,6},{2,4},{4,2},{6,0},{8,14},{10,12},{12,10},{14,8},{16,22},{18,... | collective-permute-start | bytes 1572872 | tf_op jit(solution)/shard_map/ppermute | solution.py:619
  109.1 17.6 %copy-start.1 = (f32[2,64,1024]{2,1,0:T(8,128)}, f32[2,64,1024]{2,1,0:T(8,128)S(1)}, u32[]{:S(2)}) copy-start(f32[2,64,1024]{2,1,0:T(8,128)S(1)} %collective-permute-done.6.refs_6_) | copy-start | bytes 1572868
  109.1 33.9 %collective-permute-start.27 = (f32[3,64,1024]{2,1,0:T(8,128)}, f32[3,64,1024]{2,1,0:T(8,128)}, u32[]{:S(2)}, u32[]{:S(2)}) collective-permute-start(f32[3,64,1024]{2,1,0:T(8,128)} %get-tuple-element.75), channel_id=1, source_target_pairs={{0,8},{2,10},{4,12},{6,14},{8,16},{10,18},{12,20},{14,22},{16,24},... | collective-permute-start | bytes 2359304 | tf_op jit(solution)/shard_map/ppermute | solution.py:626
  112.6 14.1 %copy-start.2 = (f32[2,64,1024]{2,1,0:T(8,128)}, f32[2,64,1024]{2,1,0:T(8,128)S(1)}, u32[]{:S(2)}) copy-start(f32[2,64,1024]{2,1,0:T(8,128)S(1)} %collective-permute-done.7.refs_7_) | copy-start | bytes 1572868
  112.6 32.8 %collective-permute-start.28 = (f32[3,64,1024]{2,1,0:T(8,128)}, f32[3,64,1024]{2,1,0:T(8,128)}, u32[]{:S(2)}, u32[]{:S(2)}) collective-permute-start(f32[3,64,1024]{2,1,0:T(8,128)} %get-tuple-element.76), channel_id=1, source_target_pairs={{8,0},{10,2},{12,4},{14,6},{16,8},{18,10},{20,12},{22,14},{24,16},... | collective-permute-start | bytes 2359304 | tf_op jit(solution)/shard_map/ppermute | solution.py:626
  115.8 10.9 %copy-start.3 = (f32[2,64,1024]{2,1,0:T(8,128)}, f32[2,64,1024]{2,1,0:T(8,128)S(1)}, u32[]{:S(2)}) copy-start(f32[2,64,1024]{2,1,0:T(8,128)S(1)} %collective-permute-done.2.refs_1_) | copy-start | bytes 1572868
  126.6 0.8 copy-start.4
  126.6 1.0 copy-start.5
  130.5 21.4 %collective-permute-start.13 = (f32[3,32,1024]{2,1,0:T(8,128)}, f32[3,32,1024]{2,1,0:T(8,128)S(1)}, u32[]{:S(2)}, u32[]{:S(2)}) collective-permute-start(f32[3,32,1024]{2,1,0:T(8,128)} %get-tuple-element.57), channel_id=1, source_target_pairs={{0,8},{2,10},{4,12},{6,14},{8,16},{10,18},{12,20},{14,22},{16,24},... | collective-permute-start | bytes 1179656 | tf_op jit(solution)/shard_map/ppermute | solution.py:626
  134.0 19.2 %collective-permute-start.14 = (f32[3,32,1024]{2,1,0:T(8,128)}, f32[3,32,1024]{2,1,0:T(8,128)S(1)}, u32[]{:S(2)}, u32[]{:S(2)}) collective-permute-start(f32[3,32,1024]{2,1,0:T(8,128)} %get-tuple-element.58), channel_id=1, source_target_pairs={{8,0},{10,2},{12,4},{14,6},{16,8},{18,10},{20,12},{22,14},{24,16},... | collective-permute-start | bytes 1179656 | tf_op jit(solution)/shard_map/ppermute | solution.py:626
  139.4 25.2 %copy-start.19 = (f32[1024,8]{1,0:T(8,128)S(1)}, f32[1024,8]{1,0:T(8,128)}, u32[]{:S(2)}) copy-start(f32[1024,8]{1,0:T(8,128)} %constant.9.clone) | copy-start | bytes 98308
  139.4 26.7 %copy-start.28 = (f32[64,10]{1,0:T(8,128)S(1)}, f32[64,10]{1,0:T(8,128)}, u32[]{:S(2)}) copy-start(f32[64,10]{1,0:T(8,128)} %constant.10.clone) | copy-start | bytes 7684
  139.4 19.8 %collective-permute-start.8 = (f32[3,32,1024]{2,1,0:T(8,128)}, f32[3,32,1024]{2,1,0:T(8,128)S(1)}, u32[]{:S(2)}, u32[]{:S(2)}) collective-permute-start(f32[3,32,1024]{2,1,0:T(8,128)} %get-tuple-element.51), channel_id=1, source_target_pairs={{0,8},{2,10},{4,12},{6,14},{8,16},{10,18},{12,20},{14,22},{16,24},... | collective-permute-start | bytes 1179656 | tf_op jit(solution)/shard_map/ppermute | solution.py:626
  143.0 17.8 %collective-permute-start.9 = (f32[3,32,1024]{2,1,0:T(8,128)}, f32[3,32,1024]{2,1,0:T(8,128)}, u32[]{:S(2)}, u32[]{:S(2)}) collective-permute-start(f32[3,32,1024]{2,1,0:T(8,128)} %get-tuple-element.52), channel_id=1, source_target_pairs={{8,0},{10,2},{12,4},{14,6},{16,8},{18,10},{20,12},{22,14},{24,16},... | collective-permute-start | bytes 1179656 | tf_op jit(solution)/shard_map/ppermute | solution.py:626
  150.3 14.3 %copy-start.27 = (f32[4,8,1024]{2,1,0:T(8,128)S(1)}, f32[4,8,1024]{2,1,0:T(8,128)}, u32[]{:S(2)}) copy-start(f32[4,8,1024]{2,1,0:T(8,128)} %get-tuple-element.81) | copy-start | bytes 393220
  150.3 52.9 %collective-permute-start.29 = (f32[3,64,1024]{2,1,0:T(8,128)}, f32[3,64,1024]{2,1,0:T(8,128)S(1)}, u32[]{:S(2)}, u32[]{:S(2)}) collective-permute-start(f32[3,64,1024]{2,1,0:T(8,128)} %get-tuple-element.78), channel_id=1, source_target_pairs={{0,2},{2,0},{4,6},{6,4},{8,10},{10,8},{12,14},{14,12},{16,18},{18,... | collective-permute-start | bytes 2359304 | tf_op jit(solution)/shard_map/ppermute | solution.py:619
  152.7 51.2 %collective-permute-start.30 = (f32[3,64,1024]{2,1,0:T(8,128)}, f32[3,64,1024]{2,1,0:T(8,128)S(1)}, u32[]{:S(2)}, u32[]{:S(2)}) collective-permute-start(f32[3,64,1024]{2,1,0:T(8,128)} %get-tuple-element.79), channel_id=1, source_target_pairs={{0,4},{2,6},{4,0},{6,2},{8,12},{10,14},{12,8},{14,10},{16,20},{18,... | collective-permute-start | bytes 2359304 | tf_op jit(solution)/shard_map/ppermute | solution.py:619
  153.9 51.7 %collective-permute-start.31 = (f32[3,64,1024]{2,1,0:T(8,128)}, f32[3,64,1024]{2,1,0:T(8,128)S(1)}, u32[]{:S(2)}, u32[]{:S(2)}) collective-permute-start(f32[3,64,1024]{2,1,0:T(8,128)} %get-tuple-element.80), channel_id=1, source_target_pairs={{0,6},{2,4},{4,2},{6,0},{8,14},{10,12},{12,10},{14,8},{16,22},{18,... | collective-permute-start | bytes 2359304 | tf_op jit(solution)/shard_map/ppermute | solution.py:619
  159.2 1.6 copy-start.20
  159.2 42.9 %collective-permute-start.15 = (f32[3,32,1024]{2,1,0:T(8,128)}, f32[3,32,1024]{2,1,0:T(8,128)}, u32[]{:S(2)}, u32[]{:S(2)}) collective-permute-start(f32[3,32,1024]{2,1,0:T(8,128)} %get-tuple-element.60), channel_id=1, source_target_pairs={{0,2},{2,0},{4,6},{6,4},{8,10},{10,8},{12,14},{14,12},{16,18},{18,... | collective-permute-start | bytes 1179656 | tf_op jit(solution)/shard_map/ppermute | solution.py:619
  166.2 1.2 collective-permute-start.32
  167.4 3.6 %collective-permute-start.33 = (f32[4,10]{1,0:T(4,128)S(1)}, f32[4,10]{1,0:T(4,128)S(1)}, u32[]{:S(2)}, u32[]{:S(2)}) collective-permute-start(f32[4,10]{1,0:T(4,128)S(1)} %add.26), channel_id=1, source_target_pairs={{0,8},{2,10},{4,12},{6,14},{8,0},{10,2},{12,4},{14,6},{16,24},{18,... | collective-permute-start | bytes 488 | tf_op jit(solution)/shard_map/ppermute | solution.py:631
  171.0 4.9 %collective-permute-start.34 = (f32[4,10]{1,0:T(4,128)S(1)}, f32[4,10]{1,0:T(4,128)S(1)}, u32[]{:S(2)}, u32[]{:S(2)}) collective-permute-start(f32[4,10]{1,0:T(4,128)S(1)} %add.27), channel_id=1, source_target_pairs={{0,16},{2,18},{4,20},{6,22},{8,24},{10,26},{12,28},{14,30},{16,0},... | collective-permute-start | bytes 488 | tf_op jit(solution)/shard_map/ppermute | solution.py:631
  175.8 16.9 %collective-permute-start.37 = (f32[4,10]{1,0:T(4,128)S(1)}, f32[4,10]{1,0:T(4,128)S(1)}, u32[]{:S(2)}, u32[]{:S(2)}) collective-permute-start(f32[4,10]{1,0:T(4,128)S(1)} %add.28), channel_id=1, source_target_pairs={{0,6},{2,4},{4,2},{6,0},{8,14},{10,12},{12,10},{14,8},{16,22},{18,... | collective-permute-start | bytes 488 | tf_op jit(solution)/shard_map/ppermute | solution.py:619
  192.7 3.7 %collective-permute-start.36 = (f32[4,10]{1,0:T(4,128)S(1)}, f32[4,10]{1,0:T(4,128)S(1)}, u32[]{:S(2)}, u32[]{:S(2)}) collective-permute-start(f32[4,10]{1,0:T(4,128)S(1)} %add.28), channel_id=1, source_target_pairs={{0,4},{2,6},{4,0},{6,2},{8,12},{10,14},{12,8},{14,10},{16,20},{18,... | collective-permute-start | bytes 488 | tf_op jit(solution)/shard_map/ppermute | solution.py:619
  196.4 3.6 %collective-permute-start.35 = (f32[4,10]{1,0:T(4,128)S(1)}, f32[4,10]{1,0:T(4,128)S(1)}, u32[]{:S(2)}, u32[]{:S(2)}) collective-permute-start(f32[4,10]{1,0:T(4,128)S(1)} %add.28), channel_id=1, source_target_pairs={{0,2},{2,0},{4,6},{6,4},{8,10},{10,8},{12,14},{14,12},{16,18},{18,... | collective-permute-start | bytes 488 | tf_op jit(solution)/shard_map/ppermute | solution.py:619
  200.1 6.8 %copy-start.30 = (f32[4,10]{1,0:T(4,128)}, f32[4,10]{1,0:T(4,128)S(1)}, u32[]{:S(2)}) copy-start(f32[4,10]{1,0:T(4,128)S(1)} %collective-permute-done.35) | copy-start | bytes 484
  200.1 24.4 %collective-permute-start.16 = (f32[3,32,1024]{2,1,0:T(8,128)}, f32[3,32,1024]{2,1,0:T(8,128)S(1)}, u32[]{:S(2)}, u32[]{:S(2)}) collective-permute-start(f32[3,32,1024]{2,1,0:T(8,128)} %get-tuple-element.61), channel_id=1, source_target_pairs={{0,4},{2,6},{4,0},{6,2},{8,12},{10,14},{12,8},{14,10},{16,20},{18,... | collective-permute-start | bytes 1179656 | tf_op jit(solution)/shard_map/ppermute | solution.py:619
  202.1 22.3 %collective-permute-start.17 = (f32[3,32,1024]{2,1,0:T(8,128)}, f32[3,32,1024]{2,1,0:T(8,128)}, u32[]{:S(2)}, u32[]{:S(2)}) collective-permute-start(f32[3,32,1024]{2,1,0:T(8,128)} %get-tuple-element.62), channel_id=1, source_target_pairs={{0,6},{2,4},{4,2},{6,0},{8,14},{10,12},{12,10},{14,8},{16,22},{18,... | collective-permute-start | bytes 1179656 | tf_op jit(solution)/shard_map/ppermute | solution.py:619
  203.3 9.2 %copy-start.15 = (f32[3,64,1024]{2,1,0:T(8,128)}, f32[3,64,1024]{2,1,0:T(8,128)S(1)}, u32[]{:S(2)}) copy-start(f32[3,64,1024]{2,1,0:T(8,128)S(1)} %collective-permute-done.29.refs_1_) | copy-start | bytes 2359300
  203.3 24.2 %collective-permute-start.10 = (f32[3,32,1024]{2,1,0:T(8,128)}, f32[3,32,1024]{2,1,0:T(8,128)S(1)}, u32[]{:S(2)}, u32[]{:S(2)}) collective-permute-start(f32[3,32,1024]{2,1,0:T(8,128)} %get-tuple-element.54), channel_id=1, source_target_pairs={{0,2},{2,0},{4,6},{6,4},{8,10},{10,8},{12,14},{14,12},{16,18},{18,... | collective-permute-start | bytes 1179656 | tf_op jit(solution)/shard_map/ppermute | solution.py:619
  203.9 8.6 %copy-start.16 = (f32[3,64,1024]{2,1,0:T(8,128)}, f32[3,64,1024]{2,1,0:T(8,128)S(1)}, u32[]{:S(2)}) copy-start(f32[3,64,1024]{2,1,0:T(8,128)S(1)} %collective-permute-done.30.refs_2_) | copy-start | bytes 2359300
  203.9 28.1 %collective-permute-start.11 = (f32[3,32,1024]{2,1,0:T(8,128)}, f32[3,32,1024]{2,1,0:T(8,128)S(1)}, u32[]{:S(2)}, u32[]{:S(2)}) collective-permute-start(f32[3,32,1024]{2,1,0:T(8,128)} %get-tuple-element.55), channel_id=1, source_target_pairs={{0,4},{2,6},{4,0},{6,2},{8,12},{10,14},{12,8},{14,10},{16,20},{18,... | collective-permute-start | bytes 1179656 | tf_op jit(solution)/shard_map/ppermute | solution.py:619
  205.6 6.9 %copy-start.17 = (f32[3,64,1024]{2,1,0:T(8,128)}, f32[3,64,1024]{2,1,0:T(8,128)S(1)}, u32[]{:S(2)}) copy-start(f32[3,64,1024]{2,1,0:T(8,128)S(1)} %collective-permute-done.31.refs_3_) | copy-start | bytes 2359300
  205.6 26.3 %collective-permute-start.12 = (f32[3,32,1024]{2,1,0:T(8,128)}, f32[3,32,1024]{2,1,0:T(8,128)}, u32[]{:S(2)}, u32[]{:S(2)}) collective-permute-start(f32[3,32,1024]{2,1,0:T(8,128)} %get-tuple-element.56), channel_id=1, source_target_pairs={{0,6},{2,4},{4,2},{6,0},{8,14},{10,12},{12,10},{14,8},{16,22},{18,... | collective-permute-start | bytes 1179656 | tf_op jit(solution)/shard_map/ppermute | solution.py:619
  209.6 2.9 %copy-start.29 = (f32[4,10]{1,0:T(4,128)S(1)}, f32[4,10]{1,0:T(4,128)}, u32[]{:S(2)}) copy-start(f32[4,10]{1,0:T(4,128)} %constant.13) | copy-start | bytes 484
  227.5 4.4 %copy-start.23 = (f32[3,32,1024]{2,1,0:T(8,128)}, f32[3,32,1024]{2,1,0:T(8,128)S(1)}, u32[]{:S(2)}) copy-start(f32[3,32,1024]{2,1,0:T(8,128)S(1)} %collective-permute-done.10.refs_1_) | copy-start | bytes 1179652
  (5 other events, 3.7 us)
